TPU v7x, 32 devices: a whole 2x2x4 slice. The times are simulated.
32 devices in a mesh: seq: 8 (over y, x, core), exp: 4 (over z).
Axes of the slice: x: 2, y: 2, z: 4, core: 2. Of those that a mesh axis runs over, the one named last changes fastest.
Arguments:
- grad_out: bfloat16 [4096, 2048], P(('seq', 'exp')), may hold values from -6 to 6
- out_proj: bfloat16 [4096, 2048], P('exp'), may hold values from -0.125 to 0.125
- step_size: float32 [64, 4096], P('exp', 'seq'), may hold values from 0.001 to 0.1
- log_decay: float32 [64, 4096], P('exp', 'seq'), may hold values from -1 to 0, as said below
- b_input: float32 [16, 4096], P(None, 'seq'), may hold values from -1.5 to 1.5
- c_output: float32 [16, 4096], P(None, 'seq'), may hold values from -1.5 to 1.5
- skip_gain: float32 [4096], P('exp'), may hold values from 0.5 to 1.5
- expert_ids: int32 [4096, 2], P('seq'), may hold values from 0 to 3, all different within a row; in each aligned block of 128 rows (0 to 127, 128 to 255, ...) at most 66 rows name the same one
- hidden_act: bfloat16 [4, 32, 66, 8192], P('exp', None, None, 'seq'), may hold values from -6 to 6
- w_down: bfloat16 [4, 8192, 2048], P('exp', 'seq'), may hold values from -0.0029296875 to 0.0029296875
Outputs:
- d_inner: bfloat16 [4096, 4096], P('seq', 'exp')
- d_gate: float32 [2, 4096], P(None, ('seq', 'exp'))
Inputs may be any that keep to these rules, and one draw needn't show every extreme that they name: `expert_ids`: each row names 2 different experts. Within the rows of one token group no expert is named by more than 66 rows, and in every draw some expert is named by exactly 66 rows of some group. `log_decay`: every entry is negative.
All inputs are finite; a program needn't handle non-finite values.
Results may differ from a plain program's by a relative error of at most 0.00065.
Values may be sent and summed in bfloat16 or wider, within the bound.
A program may use at most 128 MiB of HBM per device.

v0:
```python
import functools

import jax
import jax.numpy as jnp
from jax import lax
from jax.experimental import pallas as pl
from jax.experimental.pallas import tpu as pltpu
from jax.sharding import PartitionSpec as P

HEAD = 64


highest = lax.Precision.HIGHEST


def block_pass(state_in, pieces):
    grad_block, decay_block, step_block, b_block, c_block = pieces
    cum_decay = jnp.cumsum(decay_block, axis=1)
    gap_table = cum_decay[:, None, :] - cum_decay[:, :, None]
    upper_mask = lax.broadcasted_iota(jnp.int32, gap_table.shape, 2) >= lax.broadcasted_iota(
        jnp.int32, gap_table.shape, 1
    )
    weights = jnp.where(upper_mask, jnp.exp(jnp.where(upper_mask, gap_table, 0.0)), 0.0)
    intersection = lax.dot_general(
        b_block,
        c_block,
        (((0,), (0,)), ((), ())),
        precision=highest,
        preferred_element_type=jnp.float32,
    )
    within = jnp.einsum("hut,thp->uhp", weights * intersection[None], grad_block, precision=highest)
    tail_decay = jnp.exp(cum_decay[:, -1:] - cum_decay)
    from_state = (
        jnp.einsum("nu,hnp->uhp", b_block, state_in, precision=highest) * tail_decay.T[:, :, None]
    )
    result = step_block.T[:, :, None] * (within + from_state)
    state_out = jnp.einsum(
        "ht,nt,thp->hnp", jnp.exp(cum_decay), c_block, grad_block, precision=highest
    )
    state_out = state_out + jnp.exp(cum_decay[:, -1])[:, None, None] * state_in
    return (state_out, result)


def local_sweep(grad_rows, decay_rows, step_rows, b_rows, c_rows, start_state):
    row_count = grad_rows.shape[0]
    head_count = decay_rows.shape[0]
    block_len = min(512, row_count)
    block_count = row_count // block_len
    pieces = (
        grad_rows.reshape(block_count, block_len, head_count, grad_rows.shape[2]),
        decay_rows.reshape(head_count, block_count, block_len).transpose(1, 0, 2),
        step_rows.reshape(head_count, block_count, block_len).transpose(1, 0, 2),
        b_rows.reshape(b_rows.shape[0], block_count, block_len).transpose(1, 0, 2),
        c_rows.reshape(c_rows.shape[0], block_count, block_len).transpose(1, 0, 2),
    )
    state_out, results = lax.scan(block_pass, start_state, pieces, reverse=True)
    return (state_out, results.reshape(row_count, head_count, grad_rows.shape[2]))


def route_table(groups, expert, cap_len):
    hit_mask = jnp.any(groups == expert, axis=2)
    rank_ids = jnp.cumsum(hit_mask.astype(jnp.int32), axis=1) - 1
    slot_ids = lax.broadcasted_iota(jnp.int32, (1, 1, cap_len), 2)
    chosen = jnp.logical_and(hit_mask[:, :, None], rank_ids[:, :, None] == slot_ids)
    token_ids = lax.broadcasted_iota(jnp.int32, chosen.shape, 1)
    position = jnp.sum(jnp.where(chosen, token_ids, 0), axis=1)
    filled = jnp.any(chosen, axis=1)
    return (position, filled)


def slot_lookup(slot_table, own_ids, cap_len, expert_count):
    experts_iota = lax.broadcasted_iota(jnp.int32, (1, 1, expert_count), 2)
    onehot = own_ids[:, :, None] == experts_iota
    member = jnp.any(onehot, axis=1).astype(jnp.int32)
    rank_ids = jnp.cumsum(member, axis=0) - 1
    slot_of = jnp.sum(jnp.where(onehot, rank_ids[:, None, :], 0), axis=2)
    picked = jnp.sum(jnp.where(onehot[:, :, :, None], slot_table[None, None], 0.0), axis=2)
    slot_iota = lax.broadcasted_iota(jnp.int32, (1, 1, cap_len), 2)
    return jnp.sum(jnp.where(slot_of[:, :, None] == slot_iota, picked, 0.0), axis=2)


def shards(
    grad_out,
    out_proj,
    step_size,
    log_decay,
    b_input,
    c_output,
    skip_gain,
    expert_ids,
    hidden_act,
    w_down,
):
    exp_index = lax.axis_index("exp")
    seq_index = lax.axis_index("seq")
    exp_count = lax.axis_size("exp")
    seq_count = lax.axis_size("seq")
    tok_len = grad_out.shape[0]
    cap_len = hidden_act.shape[2]
    gathered = lax.all_gather(grad_out, "exp", axis=0, tiled=True)
    groups = expert_ids.reshape(exp_count, tok_len, expert_ids.shape[1])
    position, filled = route_table(groups, exp_index, cap_len)
    flat_index = (position + lax.broadcasted_iota(jnp.int32, position.shape, 0) * tok_len).reshape(
        -1
    )
    slot_rows = jnp.take(gathered, flat_index, axis=0)
    slot_rows = jnp.where(filled.reshape(-1, 1), slot_rows, jnp.zeros_like(slot_rows))
    saved_rows = hidden_act.reshape(-1, hidden_act.shape[3])
    weights = w_down[0]
    projected = lax.dot_general(
        lax.all_gather(slot_rows, "seq", axis=0, tiled=True),
        weights,
        (((1,), (1,)), ((), ())),
        preferred_element_type=jnp.float32,
    )
    partial_scores = jnp.sum(projected * saved_rows.astype(jnp.float32), axis=1)
    head_count = out_proj.shape[0] // HEAD
    inner_grad = lax.dot_general(
        gathered, out_proj, (((1,), (1,)), ((), ())), preferred_element_type=jnp.float32
    )
    row_count = inner_grad.shape[0]
    start_state = jnp.zeros((head_count, b_input.shape[0], HEAD), jnp.float32)
    summary, swept_part = local_sweep(
        inner_grad.reshape(row_count, head_count, HEAD),
        log_decay,
        step_size,
        b_input,
        c_output,
        start_state,
    )
    total_decay = jnp.sum(log_decay, axis=1)
    all_states, all_decay = (
        lax.all_gather(summary[None], "seq", axis=0, tiled=True),
        lax.all_gather(total_decay[None], "seq", axis=0, tiled=True),
    )
    shard_ids = lax.broadcasted_iota(jnp.int32, all_decay.shape, 0)
    beyond = jnp.where(shard_ids > seq_index, all_decay, 0.0)
    exponent = jnp.cumsum(beyond, axis=0) - beyond
    factor = jnp.where(
        shard_ids > seq_index, jnp.exp(jnp.where(shard_ids > seq_index, exponent, 0.0)), 0.0
    )
    incoming = jnp.sum(factor[:, :, None, None] * all_states, axis=0)
    suffix = jnp.flip(jnp.cumsum(jnp.flip(log_decay, 1), axis=1), 1) - log_decay
    from_carry = (
        jnp.einsum("nu,hnp->uhp", b_input, incoming, precision=highest)
        * jnp.exp(suffix).T[:, :, None]
    )
    combined = swept_part + step_size.T[:, :, None] * from_carry
    d_inner = (combined.reshape(row_count, -1) + skip_gain * inner_grad).astype(jnp.bfloat16)
    summed = lax.psum_scatter(
        partial_scores.reshape(seq_count, exp_count, cap_len),
        "seq",
        scatter_dimension=0,
        tiled=True,
    )
    slot_table = lax.all_to_all(
        summed.reshape(exp_count, 1, cap_len), "exp", split_axis=0, concat_axis=1, tiled=True
    ).reshape(exp_count, cap_len)
    own_ids = lax.dynamic_slice_in_dim(expert_ids, exp_index * tok_len, tok_len, 0)
    d_gate = slot_lookup(slot_table, own_ids, cap_len, exp_count).T
    return (d_inner, d_gate)


VMEM_ROOM = 60 << 20
BF = jnp.bfloat16
F32 = jnp.float32


def halves(x):
    top = x.astype(BF)
    return top, (x - top.astype(F32)).astype(BF)


def dot(x, y, dims=((1,), (0,)), precision=None):
    return lax.dot_general(x, y, (dims, ((), ())), precision=precision, preferred_element_type=F32)


def flip(index, bit):
    return index + bit - 2 * bit * ((index // bit) % 2)


def column(table, h):
    lanes = lax.broadcasted_iota(jnp.int32, table.shape, 1)
    return jnp.sum(jnp.where(lanes == h, table, 0.0), axis=1, keepdims=True)


def fused(
    sizes,
    grad_hbm, proj_hbm, hid_hbm, down_hbm, step_ref, decay_ref, b_ref, c_ref, skip_ref, ids_ref,
    out_ref, table_ref,
    gath, proj, hid, down, y_ref, rows, pick, inner, fac, acc,
    cum_ref, cum_t, step_t, b_t, bc, agg, got, carry, mail, inbox,
    load_sem, hid_sem, down_sem, proj_sem,
    zs_sem, zr_sem, xs_sem, xr_sem, as_sem, ar_sem, ms_sem, mr_sem,
):
    n_seq, n_exp, tok, cap, shard, chunks, width = sizes
    me = lax.axis_index("seq")
    z = lax.axis_index("exp")
    row_count = n_exp * tok
    spread = 2 * n_exp
    n_dev = n_seq * n_exp
    mine_id = me * n_exp + z
    bits = [1 << i for i in range(1, n_seq.bit_length() - 1)]
    n_stage = len(bits)
    steps = n_exp - 1
    block = bc.shape[1]
    blocks = row_count // block
    channels = inner.shape[1]
    lane = 2 * HEAD
    pairs = channels // lane

    for k in range(chunks):
        pltpu.make_async_copy(
            grad_hbm.at[:, pl.ds(k * width, width)], gath.at[k, z], load_sem.at[k]
        ).start()
    down_copy = pltpu.make_async_copy(down_hbm.at[0], down, down_sem)
    down_copy.start()
    hid_copy = pltpu.make_async_copy(hid_hbm.at[0], hid, hid_sem)
    hid_copy.start()
    for k in range(chunks):
        pltpu.make_async_copy(
            proj_hbm.at[:, pl.ds(k * width, width)], proj.at[k], proj_sem.at[k]
        ).start()

    barrier = pltpu.get_barrier_semaphore()

    def greet(i, _):
        other = lax.rem(mine_id + i, n_dev)
        pl.semaphore_signal(
            barrier, inc=1, device_id={"seq": other // n_exp, "exp": lax.rem(other, n_exp)}
        )
        return 0

    lax.fori_loop(1, n_dev, greet, 0)
    pl.semaphore_wait(barrier, n_dev - 1)

    def z_copy(side, k, d, owner, target):
        return pltpu.make_async_remote_copy(
            src_ref=gath.at[k, owner],
            dst_ref=gath.at[k, owner],
            send_sem=zs_sem.at[side, k, d],
            recv_sem=zr_sem.at[side, k, d],
            device_id={"exp": target},
        )

    def z_send(k, d):
        @pl.when(jnp.logical_and(z < n_exp - 1, z - d >= 0))
        def _():
            z_copy(0, k, d, z - d, z + 1).start()

        @pl.when(jnp.logical_and(z > 0, z + d < n_exp))
        def _():
            z_copy(1, k, d, z + d, z - 1).start()

    def z_sent(k, d):
        @pl.when(jnp.logical_and(z < n_exp - 1, z - d >= 0))
        def _():
            z_copy(0, k, d, z - d, z + 1).wait_send()

        @pl.when(jnp.logical_and(z > 0, z + d < n_exp))
        def _():
            z_copy(1, k, d, z + d, z - 1).wait_send()

    def z_take(k, d):
        @pl.when(z - d >= 0)
        def _():
            z_copy(0, k, d - 1, z - d, z).wait_recv()

        @pl.when(z + d < n_exp)
        def _():
            z_copy(1, k, d - 1, z + d, z).wait_recv()

    for k in range(chunks):
        pltpu.make_async_copy(
            grad_hbm.at[:, pl.ds(k * width, width)], gath.at[k, z], load_sem.at[k]
        ).wait()
        if k == 0:
            z_send(k, 0)

    def bit_of(k, stage):
        if stage == n_stage:
            return 1
        low, high = bits[stage], bits[n_stage - 1 - stage]
        return low + (high - low) * (k % 2)

    def x_copies(k, stage, here):
        masks = [()]
        for i in range(stage):
            masks = masks + [m + (i,) for m in masks]
        copies = []
        for j, mask in enumerate(masks):
            owner = me
            for i in mask:
                owner = flip(owner, bit_of(k, i))
            slot = (1 << stage) - 1 + j
            if not here:
                owner = flip(owner, bit_of(k, stage))
            copies.append(pltpu.make_async_remote_copy(
                src_ref=rows.at[k, owner],
                dst_ref=rows.at[k, owner],
                send_sem=xs_sem.at[k, slot],
                recv_sem=xr_sem.at[k, slot],
                device_id={"seq": flip(me, bit_of(k, stage))},
            ))
        return copies

    def x_start(k, stage):
        for mine in x_copies(k, stage, True):
            mine.start()

    def x_take(k, stage):
        for theirs in x_copies(k, stage, False):
            theirs.wait_recv()

    hit = jnp.zeros((1, row_count), F32)
    for i in range(ids_ref.shape[0]):
        hit = jnp.maximum(hit, jnp.where(ids_ref[i : i + 1, :] == z, 1.0, 0.0))
    row_id = lax.broadcasted_iota(jnp.int32, (row_count, row_count), 0)
    col_id = lax.broadcasted_iota(jnp.int32, (row_count, row_count), 1)
    same = jnp.logical_and(row_id // tok == col_id // tok, row_id < col_id)
    before = dot(jnp.broadcast_to(hit, (16, row_count)).astype(BF), jnp.where(same, 1.0, 0.0).astype(BF))
    group = lax.broadcasted_iota(jnp.int32, (1, row_count), 1) // tok
    place = before[0:1].astype(jnp.int32) * n_exp + group
    place = jnp.where(hit > 0.5, place, -1)
    chosen = lax.broadcasted_iota(jnp.int32, (shard, row_count), 0) == place
    pick[...] = jnp.where(chosen, 1.0, 0.0).astype(BF)

    tri = jnp.where(row_id <= col_id, 1.0, 0.0)
    cum = dot(decay_ref[...], tri, precision=highest)
    cum_ref[...] = cum
    cum_t[...] = jnp.transpose(cum)
    step_t[...] = jnp.transpose(step_ref[...])
    b_t[...] = jnp.transpose(b_ref[...])
    keep = lax.broadcasted_iota(jnp.int32, (block, block), 1) >= lax.broadcasted_iota(
        jnp.int32, (block, block), 0
    )
    for i in range(blocks):
        span = slice(i * block, (i + 1) * block)
        cross = dot(b_t[span, :], c_ref[:, span], precision=highest)
        bc[i] = jnp.where(keep, cross, 0.0)

    inner[...] = jnp.zeros_like(inner)
    acc[...] = jnp.zeros_like(acc)
    down_copy.wait()
    hid_copy.wait()

    group_count = hid.shape[1]
    span_c = max(c for c in range(1, cap + 1) if cap % c == 0 and c * group_count <= 384)
    parts_c = cap // span_c

    def project(i):
        span = pl.ds(i * span_c, span_c)
        saved = hid[span].reshape(span_c * group_count, hid.shape[2])
        for k in range(chunks):
            part = dot(saved, down[:, k * width : (k + 1) * width])
            y_ref[k, span] = part.reshape(span_c, group_count, width)

    def z_step(i, _):
        k, d = i // steps, i % steps + 1
        z_take(k, d)

        @pl.when(d < steps)
        def _():
            z_send(k, d)

        @pl.when(jnp.logical_and(d == 1, k < chunks - 1))
        def _():
            z_send(k + 1, 0)

        @pl.when(jnp.logical_and(d == 1, k >= 2))
        def _():
            x_take(k - 2, 1)
            x_start(k - 2, 2)

        @pl.when(jnp.logical_and(d == 2, k >= 1))
        def _():
            x_take(k - 1, 0)
            x_start(k - 1, 1)

        @pl.when(jnp.logical_and(d == 1, k < parts_c))
        def _():
            project(k)

        @pl.when(d == steps)
        def _():
            block_in = gath[k].reshape(row_count, width)
            rows[k, me] = dot(pick[...], block_in).astype(BF)
            x_start(k, 0)
            pltpu.make_async_copy(
                proj_hbm.at[:, pl.ds(0, width)], proj.at[k], proj_sem.at[k]
            ).wait()
            inner[...] += dot(block_in, proj[k], ((1,), (1,)))

        return 0

    lax.fori_loop(0, chunks * steps, z_step, 0)
    for i in range(chunks, parts_c):
        project(i)

    left_of = lax.broadcasted_iota(jnp.int32, (1, lane), 1) < HEAD

    def pair_step(j, _):
        span = pl.ds(pl.multiple_of(j * lane, lane), lane)
        cols = [column(cum_t[...], 2 * j + i) for i in range(2)]
        rowv = [cum_ref[pl.ds(2 * j + i, 1), :] for i in range(2)]
        steps_col = jnp.where(
            left_of, column(step_t[...], 2 * j), column(step_t[...], 2 * j + 1)
        )
        col = jnp.where(left_of, cols[0], cols[1])
        end_row = jnp.where(left_of, cols[0][row_count - 1 :], cols[1][row_count - 1 :])
        fac[:, span] = steps_col * jnp.exp(end_row - col)
        skip = skip_ref[:, span]
        state = jnp.zeros((b_t.shape[1], lane), F32)
        for i in reversed(range(blocks)):
            lo, hi = i * block, (i + 1) * block
            g = inner[lo:hi, span]
            g_top, g_low = halves(g)
            both = jnp.concatenate([g_top, g_low], axis=1)
            parts, sums = [], []
            for q in range(2):
                r = rowv[q][:, lo:hi]
                w = jnp.exp(jnp.minimum(r - cols[q][lo:hi], 0.0)) * bc[i]
                w_top, w_low = halves(w)
                x = dot(w_top, both)
                parts.append(x[:, :lane] + x[:, lane:] + dot(w_low, g_top))
                base = rowv[q][:, lo - 1 : lo] if i else jnp.zeros((1, 1), F32)
                m_top, m_low = halves(c_ref[:, lo:hi] * jnp.exp(r - base))
                x = dot(m_top, both)
                sums.append(x[:, :lane] + x[:, lane:] + dot(m_low, g_top))
            result = jnp.where(left_of, parts[0], parts[1])
            if i < blocks - 1:
                edge = col[hi - 1 : hi]
                result += jnp.exp(edge - col[lo:hi]) * dot(b_t[lo:hi, :], state, precision=highest)
            start = col[lo - 1 : lo] if i else jnp.zeros((1, lane), F32)
            state = jnp.where(left_of, sums[0], sums[1]) + jnp.exp(col[hi - 1 : hi] - start) * state
            inner[lo:hi, span] = steps_col[lo:hi] * result + skip * g
        agg[0, : b_t.shape[1], span] = state
        agg[0, b_t.shape[1] :, span] = jnp.broadcast_to(end_row, (8, lane))
        return 0

    low_half = lax.broadcasted_iota(jnp.int32, (1, spread, width), 1) < n_exp

    def scores(k):
        def one(p, _):
            first = rows[k, 2 * p][: cap * n_exp].astype(F32).reshape(cap // 2, spread, width)
            second = rows[k, 2 * p + 1][: cap * n_exp].astype(F32).reshape(cap // 2, spread, width)
            even = jnp.where(low_half, first, pltpu.roll(second, n_exp, 1))
            odd = jnp.where(low_half, pltpu.roll(first, n_exp, 1), second)
            y = y_ref[k, :, pl.ds(pl.multiple_of(p * spread, spread), spread), :]
            y = y.reshape(cap // 2, 2, spread, width)
            for i, part in enumerate((even * y[:, 0], odd * y[:, 1])):
                total = part[:, :, :128]
                for j in range(1, width // 128):
                    total = total + part[:, :, j * 128 : (j + 1) * 128]
                acc[p, :, i] += total
            return 0

        lax.fori_loop(0, n_seq // 2, one, 0)

    tasks = []
    for stage in range(1, n_stage + 1):
        for k in range(chunks):
            if k + stage >= chunks:
                tasks.append((k, stage))
    tasks.sort(key=lambda t: (t[0] + 1.5 * t[1], t[0]))

    def serve(count):
        for _ in range(min(count, len(tasks))):
            k, stage = tasks.pop(0)
            x_take(k, stage - 1)
            x_start(k, stage)

    cut = pairs // 2
    lax.fori_loop(0, cut, pair_step, 0)
    serve(1)
    lax.fori_loop(cut, pairs, pair_step, 0)

    n_state = b_t.shape[1]
    carry[...] = jnp.zeros_like(carry)
    reach = jnp.zeros((1, channels), F32)

    def a_copy(i, bit):
        return pltpu.make_async_remote_copy(
            src_ref=agg.at[i],
            dst_ref=got.at[i],
            send_sem=as_sem.at[i],
            recv_sem=ar_sem.at[i],
            device_id={"seq": flip(me, bit)},
        )

    order = [1] + bits
    a_copy(0, 1).start()
    for i, bit in enumerate(order):
        if i == 0:
            serve(1)
        while (i, n_stage) in tasks:
            serve(1)
        x_take(i, n_stage)
        scores(i)
        a_copy(i, bit).wait_recv()
        low = ((me // bit) % 2) == 0
        other, other_t = got[i, :n_state, :], got[i, n_state : n_state + 1, :]
        own, own_t = agg[i, :n_state, :], agg[i, n_state : n_state + 1, :]
        carry[...] += jnp.where(low, jnp.exp(reach) * other, 0.0)
        reach = reach + jnp.where(low, other_t, 0.0)
        if i + 1 < len(order):
            first = jnp.where(low, own, other)
            first_t = jnp.where(low, own_t, other_t)
            second = jnp.where(low, other, own)
            agg[i + 1, :n_state, :] = first + jnp.exp(first_t) * second
            agg[i + 1, n_state:, :] = jnp.broadcast_to(own_t + other_t, (8, channels))
            a_copy(i + 1, order[i + 1]).start()

    for i in range(blocks):
        lo, hi = i * block, (i + 1) * block
        from_carry = dot(b_t[lo:hi, :], carry[...], precision=highest)
        out_ref[lo:hi, :] = (inner[lo:hi, :] + fac[lo:hi, :] * from_carry).astype(BF)

    for k in range(len(order), chunks):
        if k >= chunks - 2:
            serve(len(tasks))
        x_take(k, n_stage)
        scores(k)

    def finish(p, _):
        wide = jnp.transpose(acc[p].reshape(cap * spread, 128))
        mail[p] = jnp.sum(wide, axis=0, keepdims=True)
        return 0

    lax.fori_loop(0, n_seq // 2, finish, 0)

    def mail_copy(other, source, slot):
        return pltpu.make_async_remote_copy(
            src_ref=mail.at[other // spread],
            dst_ref=inbox.at[source],
            send_sem=ms_sem.at[slot],
            recv_sem=mr_sem.at[source],
            device_id={"seq": other // n_exp, "exp": lax.rem(other, n_exp)},
        )

    def post(i, _):
        other = lax.rem(mine_id + i, n_dev)
        mail_copy(other, mine_id, other).start()
        return 0

    def take(i, _):
        other = lax.rem(mine_id + i, n_dev)
        mail_copy(other, other, other).wait_recv()
        return 0

    def posted(i, _):
        other = lax.rem(mine_id + i, n_dev)
        mail_copy(other, mine_id, other).wait_send()
        return 0

    lax.fori_loop(1, n_dev, post, 0)
    inbox[mine_id] = mail[me // 2]
    lax.fori_loop(1, n_dev, take, 0)
    for e in range(n_exp):
        total = inbox[e]
        for i in range(1, n_seq):
            total = total + inbox[i * n_exp + e]
        table_ref[e] = total
    lax.fori_loop(1, n_dev, posted, 0)

    for k in range(chunks):
        for d in range(steps):
            z_sent(k, d)
        for stage in range(n_stage + 1):
            for mine in x_copies(k, stage, True):
                mine.wait_send()
    for i, bit in enumerate(order):
        a_copy(i, bit).wait_send()


def plan(n_seq, n_exp, tok, depth, channels, cap, hidden, state):
    chunks = 8
    width = depth // chunks
    shard = -(-cap * n_exp // 16) * 16
    row_count = n_exp * tok
    letter = cap * n_exp * 2
    block = min(256, row_count)
    heads = channels // HEAD
    stages = n_seq.bit_length() - 1
    steps = n_exp - 1
    shapes = [
        ((chunks, n_exp, tok, width), BF),
        ((chunks, channels, width), BF),
        ((cap, n_seq * n_exp, hidden), BF),
        ((hidden, depth), BF),
        ((chunks, cap, n_seq * n_exp, width), F32),
        ((chunks, n_seq, shard, width), BF),
        ((shard, row_count), BF),
        ((row_count, channels), F32),
        ((row_count, channels), F32),
        ((n_seq // 2, cap // 2, 2, 2 * n_exp, 128), F32),
        ((heads, row_count), F32),
        ((row_count, heads), F32),
        ((row_count, heads), F32),
        ((row_count, state), F32),
        ((row_count // block, block, block), F32),
        ((stages, state + 8, channels), F32),
        ((stages, state + 8, channels), F32),
        ((state, channels), F32),
        ((n_seq // 2, 1, letter), F32),
        ((n_seq * n_exp, 1, letter), F32),
    ]
    total = 0
    for shape, kind in shapes:
        size = 1
        for extent in shape:
            size *= extent
        total += size * (2 if kind is BF else 4)
    fits = (
        total < VMEM_ROOM - (8 << 20)
        and n_seq & (n_seq - 1) == 0
        and stages == 3
        and n_exp == 4
        and cap % 2 == 0
        and depth % (128 * chunks) == 0
        and channels % (2 * HEAD) == 0
        and row_count % block == 0
        and tok % 8 == 0
    )
    sems = [
        (chunks,), (), (), (chunks,),
        (2, chunks, steps), (2, chunks, steps),
        (chunks, n_seq - 1), (chunks, n_seq - 1),
        (stages,), (stages,),
        (n_seq * n_exp,), (n_seq * n_exp,),
    ]
    return fits, (n_seq, n_exp, tok, cap, shard, chunks, width), shapes, sems


def quick(
    fitted, grad_out, out_proj, step_size, log_decay, b_input, c_output, skip_gain, expert_ids,
    hidden_act, w_down,
):
    _, sizes, shapes, sems = fitted
    n_seq, n_exp, tok, cap, shard, chunks, width = sizes
    vmem = pl.BlockSpec(memory_space=pltpu.VMEM)
    hbm = pl.BlockSpec(memory_space=pl.ANY)
    row_count, channels = n_exp * tok, out_proj.shape[0]
    d_inner, table = pl.pallas_call(
        functools.partial(fused, sizes),
        out_shape=(
            jax.ShapeDtypeStruct((row_count, channels), BF),
            jax.ShapeDtypeStruct((n_exp, 1, 2 * n_exp * cap), F32),
        ),
        in_specs=[hbm] * 4 + [vmem] * 6,
        out_specs=(vmem, vmem),
        scratch_shapes=[pltpu.VMEM(shape, kind) for shape, kind in shapes]
        + [pltpu.SemaphoreType.DMA(s) if s else pltpu.SemaphoreType.DMA for s in sems],
        compiler_params=pltpu.CompilerParams(
            collective_id=0, has_side_effects=True, vmem_limit_bytes=VMEM_ROOM
        ),
    )(
        grad_out, out_proj, hidden_act.transpose(0, 2, 1, 3), w_down, step_size, log_decay, b_input, c_output,
        skip_gain.reshape(1, -1), expert_ids.T,
    )
    exp_index = lax.axis_index("exp")
    own_ids = lax.dynamic_slice_in_dim(expert_ids, exp_index * tok, tok, 0)
    group = lax.rem(lax.axis_index("seq"), 2) * n_exp + exp_index
    experts = lax.broadcasted_iota(jnp.int32, (1, 1, n_exp), 2)
    onehot = own_ids[:, :, None] == experts
    member = jnp.any(onehot, axis=1).astype(jnp.int32)
    rank_ids = jnp.cumsum(member, axis=0) - 1
    slot_of = jnp.sum(jnp.where(onehot, rank_ids[:, None, :], 0), axis=2)
    spot = own_ids * table.shape[2] + slot_of * (2 * n_exp) + group
    flat = table.reshape(1, 1, -1)
    spots = lax.broadcasted_iota(jnp.int32, flat.shape, 2)
    d_gate = jnp.sum(jnp.where(spots == spot.T[:, :, None], flat, 0.0), axis=2)
    return d_inner, d_gate


def route(*args):
    grad_out, out_proj, step_size, log_decay, b_input, c_output, skip_gain, ids, hidden, down = args
    fitted = plan(
        lax.axis_size("seq"), lax.axis_size("exp"), grad_out.shape[0], grad_out.shape[1],
        out_proj.shape[0], hidden.shape[2], hidden.shape[3], b_input.shape[0],
    )
    if fitted[0]:
        return quick(fitted, *args)
    return shards(*args)


def solution(mesh):
    in_specs = (
        P(("seq", "exp"), None),
        P("exp", None),
        P("exp", "seq"),
        P("exp", "seq"),
        P(None, "seq"),
        P(None, "seq"),
        P("exp"),
        P("seq", None),
        P("exp", None, None, "seq"),
        P("exp", "seq", None),
    )
    out_specs = (P("seq", "exp"), P(None, ("seq", "exp")))
    return jax.shard_map(route, mesh=mesh, in_specs=in_specs, out_specs=out_specs, check_vma=False)
```

profile of v0, /device:TPU:0, one launch (start us, length us, event | category | flops | bytes accessed | tf_op | source)
XLA Modules:
  0.0 107.5 jit_solution(10073882231246933455)
XLA Ops:
  0.6 0.7 constant_dynamic-slice_fusion
  1.3 0.1 copy.13
  1.5 0.2 reduce_window_sum.11
  1.6 0.1 copy.14
  1.7 0.7 add_bitcast_fusion
  2.4 101.1 %shard_map.113 = (bf16[512,1024]{1,0:T(8,128)(2,1)}, f32[4,1,528]{2,1,0:T(1,128)}) custom-call(bf16[128,2048]{1,0:T(8,128)(2,1)} %grad_hbm.1, bf16[1024,2048]{1,0:T(8,128)(2,1)} %proj_hbm.1, bf16[1,66,32,1024]{3,2,1,0:T(8,128)(2,1)} %bitcast.5, bf16[1,1024,2048]{2,1,0:T(8,128)(2,1)} %down_hbm.1, f32[16,512]{1,0:T(8,128)} %step_ref.1, f32[16,512]{1,0:T(8,128)} %decay_ref.1, ...), custom_call_target="tpu_custom_call" | custom-call | tf_op jit(solution)/shard_map/pallas_call | solution.py:644
  103.5 0.7 reduce
  104.2 0.1 broadcast_in_dim.31
  104.3 0.9 select_reduce_fusion
  105.3 2.3 %copy.16 = bf16[512,1024]{1,0:T(8,128)(2,1)} copy(bf16[512,1024]{1,0:T(8,128)(2,1)} %get-tuple-element.8) | data formatting | bytes 2097152
  (4 shorter events, 0.1 us)
where the time goes:
time: 108 us
  Pallas kernels  101 us (94%)
  local copies, waits for them, and re-layouts  3.2 us (3%)
  other arithmetic  2.59 us (2%)
    pallas_call x1, Pallas kernels, quick(): pl.pallas_call(functools.partial(fused, sizes), out_shape=(jax.ShapeDtype...  101 us
    unnamed x1, local copies, waits for them, and re-layouts  2.26 us

commit v1 on v0

v1 whole, which is shorter than its diff:
```python
import functools

import jax
import jax.numpy as jnp
from jax import lax
from jax.experimental import pallas as pl
from jax.experimental.pallas import tpu as pltpu
from jax.sharding import PartitionSpec as P

HEAD = 64


highest = lax.Precision.HIGHEST


def block_pass(state_in, pieces):
    grad_block, decay_block, step_block, b_block, c_block = pieces
    cum_decay = jnp.cumsum(decay_block, axis=1)
    gap_table = cum_decay[:, None, :] - cum_decay[:, :, None]
    upper_mask = lax.broadcasted_iota(jnp.int32, gap_table.shape, 2) >= lax.broadcasted_iota(
        jnp.int32, gap_table.shape, 1
    )
    weights = jnp.where(upper_mask, jnp.exp(jnp.where(upper_mask, gap_table, 0.0)), 0.0)
    intersection = lax.dot_general(
        b_block,
        c_block,
        (((0,), (0,)), ((), ())),
        precision=highest,
        preferred_element_type=jnp.float32,
    )
    within = jnp.einsum("hut,thp->uhp", weights * intersection[None], grad_block, precision=highest)
    tail_decay = jnp.exp(cum_decay[:, -1:] - cum_decay)
    from_state = (
        jnp.einsum("nu,hnp->uhp", b_block, state_in, precision=highest) * tail_decay.T[:, :, None]
    )
    result = step_block.T[:, :, None] * (within + from_state)
    state_out = jnp.einsum(
        "ht,nt,thp->hnp", jnp.exp(cum_decay), c_block, grad_block, precision=highest
    )
    state_out = state_out + jnp.exp(cum_decay[:, -1])[:, None, None] * state_in
    return (state_out, result)


def local_sweep(grad_rows, decay_rows, step_rows, b_rows, c_rows, start_state):
    row_count = grad_rows.shape[0]
    head_count = decay_rows.shape[0]
    block_len = min(512, row_count)
    block_count = row_count // block_len
    pieces = (
        grad_rows.reshape(block_count, block_len, head_count, grad_rows.shape[2]),
        decay_rows.reshape(head_count, block_count, block_len).transpose(1, 0, 2),
        step_rows.reshape(head_count, block_count, block_len).transpose(1, 0, 2),
        b_rows.reshape(b_rows.shape[0], block_count, block_len).transpose(1, 0, 2),
        c_rows.reshape(c_rows.shape[0], block_count, block_len).transpose(1, 0, 2),
    )
    state_out, results = lax.scan(block_pass, start_state, pieces, reverse=True)
    return (state_out, results.reshape(row_count, head_count, grad_rows.shape[2]))


def route_table(groups, expert, cap_len):
    hit_mask = jnp.any(groups == expert, axis=2)
    rank_ids = jnp.cumsum(hit_mask.astype(jnp.int32), axis=1) - 1
    slot_ids = lax.broadcasted_iota(jnp.int32, (1, 1, cap_len), 2)
    chosen = jnp.logical_and(hit_mask[:, :, None], rank_ids[:, :, None] == slot_ids)
    token_ids = lax.broadcasted_iota(jnp.int32, chosen.shape, 1)
    position = jnp.sum(jnp.where(chosen, token_ids, 0), axis=1)
    filled = jnp.any(chosen, axis=1)
    return (position, filled)


def slot_lookup(slot_table, own_ids, cap_len, expert_count):
    experts_iota = lax.broadcasted_iota(jnp.int32, (1, 1, expert_count), 2)
    onehot = own_ids[:, :, None] == experts_iota
    member = jnp.any(onehot, axis=1).astype(jnp.int32)
    rank_ids = jnp.cumsum(member, axis=0) - 1
    slot_of = jnp.sum(jnp.where(onehot, rank_ids[:, None, :], 0), axis=2)
    picked = jnp.sum(jnp.where(onehot[:, :, :, None], slot_table[None, None], 0.0), axis=2)
    slot_iota = lax.broadcasted_iota(jnp.int32, (1, 1, cap_len), 2)
    return jnp.sum(jnp.where(slot_of[:, :, None] == slot_iota, picked, 0.0), axis=2)


def shards(
    grad_out,
    out_proj,
    step_size,
    log_decay,
    b_input,
    c_output,
    skip_gain,
    expert_ids,
    hidden_act,
    w_down,
):
    exp_index = lax.axis_index("exp")
    seq_index = lax.axis_index("seq")
    exp_count = lax.axis_size("exp")
    seq_count = lax.axis_size("seq")
    tok_len = grad_out.shape[0]
    cap_len = hidden_act.shape[2]
    gathered = lax.all_gather(grad_out, "exp", axis=0, tiled=True)
    groups = expert_ids.reshape(exp_count, tok_len, expert_ids.shape[1])
    position, filled = route_table(groups, exp_index, cap_len)
    flat_index = (position + lax.broadcasted_iota(jnp.int32, position.shape, 0) * tok_len).reshape(
        -1
    )
    slot_rows = jnp.take(gathered, flat_index, axis=0)
    slot_rows = jnp.where(filled.reshape(-1, 1), slot_rows, jnp.zeros_like(slot_rows))
    saved_rows = hidden_act.reshape(-1, hidden_act.shape[3])
    weights = w_down[0]
    projected = lax.dot_general(
        lax.all_gather(slot_rows, "seq", axis=0, tiled=True),
        weights,
        (((1,), (1,)), ((), ())),
        preferred_element_type=jnp.float32,
    )
    partial_scores = jnp.sum(projected * saved_rows.astype(jnp.float32), axis=1)
    head_count = out_proj.shape[0] // HEAD
    inner_grad = lax.dot_general(
        gathered, out_proj, (((1,), (1,)), ((), ())), preferred_element_type=jnp.float32
    )
    row_count = inner_grad.shape[0]
    start_state = jnp.zeros((head_count, b_input.shape[0], HEAD), jnp.float32)
    summary, swept_part = local_sweep(
        inner_grad.reshape(row_count, head_count, HEAD),
        log_decay,
        step_size,
        b_input,
        c_output,
        start_state,
    )
    total_decay = jnp.sum(log_decay, axis=1)
    all_states, all_decay = (
        lax.all_gather(summary[None], "seq", axis=0, tiled=True),
        lax.all_gather(total_decay[None], "seq", axis=0, tiled=True),
    )
    shard_ids = lax.broadcasted_iota(jnp.int32, all_decay.shape, 0)
    beyond = jnp.where(shard_ids > seq_index, all_decay, 0.0)
    exponent = jnp.cumsum(beyond, axis=0) - beyond
    factor = jnp.where(
        shard_ids > seq_index, jnp.exp(jnp.where(shard_ids > seq_index, exponent, 0.0)), 0.0
    )
    incoming = jnp.sum(factor[:, :, None, None] * all_states, axis=0)
    suffix = jnp.flip(jnp.cumsum(jnp.flip(log_decay, 1), axis=1), 1) - log_decay
    from_carry = (
        jnp.einsum("nu,hnp->uhp", b_input, incoming, precision=highest)
        * jnp.exp(suffix).T[:, :, None]
    )
    combined = swept_part + step_size.T[:, :, None] * from_carry
    d_inner = (combined.reshape(row_count, -1) + skip_gain * inner_grad).astype(jnp.bfloat16)
    summed = lax.psum_scatter(
        partial_scores.reshape(seq_count, exp_count, cap_len),
        "seq",
        scatter_dimension=0,
        tiled=True,
    )
    slot_table = lax.all_to_all(
        summed.reshape(exp_count, 1, cap_len), "exp", split_axis=0, concat_axis=1, tiled=True
    ).reshape(exp_count, cap_len)
    own_ids = lax.dynamic_slice_in_dim(expert_ids, exp_index * tok_len, tok_len, 0)
    d_gate = slot_lookup(slot_table, own_ids, cap_len, exp_count).T
    return (d_inner, d_gate)


VMEM_ROOM = 63 << 20
BF = jnp.bfloat16
F32 = jnp.float32
LAG_FIRST = 2
LAG_SECOND = 4
scope = jax.named_scope


def halves(x):
    top = x.astype(BF)
    return top, (x - top.astype(F32)).astype(BF)


def dot(x, y, dims=((1,), (0,)), precision=None):
    return lax.dot_general(x, y, (dims, ((), ())), precision=precision, preferred_element_type=F32)


def flip(index, bit):
    return index + bit - 2 * bit * ((index // bit) % 2)


def column(table, h):
    lanes = lax.broadcasted_iota(jnp.int32, table.shape, 1)
    return jnp.sum(jnp.where(lanes == h, table, 0.0), axis=1, keepdims=True)


def nearest(z, i):
    upper = z // 2
    low = z + upper * (3 - 2 * z)
    group = i + low * (1 - i // 2) * (1 - 2 * i)
    return group + upper * (3 - 2 * group)


def turn_of(z, group):
    upper = z // 2
    low = z + upper * (3 - 2 * z)
    mirrored = group + upper * (3 - 2 * group)
    return mirrored + low * (1 - mirrored // 2) * (1 - 2 * mirrored)


def fused(
    sizes,
    grad_hbm, proj_hbm, hid_hbm, down_hbm, step_ref, decay_ref, b_ref, c_ref, skip_ref, ids_ref,
    out_ref, gate_ref,
    gath, proj, hid, down, turned, y_ref, y_tail, rows, tail, pick, pick_tail, inner, fac, fac_mid,
    acc, acc_tail, cum_ref, cum_t, step_t, b_t, bc, mix, lead, mid, span_sum, span_got, agg, got,
    carry, spot, mail, inbox, vals,
    load_sem, hid_sem, down_sem, proj_sem,
    zs_sem, zr_sem, xs_sem, xr_sem, ds_sem, dr_sem, as_sem, ar_sem, ms_sem, mr_sem,
):
    n_seq, n_exp, tok, cap, parts, width = sizes
    me = lax.axis_index("seq")
    z = lax.axis_index("exp")
    row_count = n_exp * tok
    n_dev = n_seq * n_exp
    mine_id = me * n_exp + z
    bits = [1 << i for i in range(1, n_seq.bit_length() - 1)]
    order = [1] + bits
    n_stage = len(bits)
    block = bc.shape[1]
    blocks = row_count // block
    channels = inner.shape[1]
    lane = 2 * HEAD
    pairs = channels // lane
    main = y_ref.shape[2]
    extra = cap - main
    half_w = width // 2
    units = n_exp * parts
    n_state = b_t.shape[1]

    for k in range(parts):
        pltpu.make_async_copy(
            grad_hbm.at[:, pl.ds(k * width, width)], gath.at[k, z], load_sem.at[k]
        ).start()
    hid_copy = pltpu.make_async_copy(hid_hbm.at[0], hid, hid_sem)
    hid_copy.start()
    for k in range(parts):
        pltpu.make_async_copy(
            down_hbm.at[0, :, pl.ds(k * width, width)], down.at[k], down_sem.at[k]
        ).start()
    for k in range(parts):
        pltpu.make_async_copy(
            proj_hbm.at[:, pl.ds(k * width, width)], proj.at[k], proj_sem.at[k]
        ).start()

    barrier = pltpu.get_barrier_semaphore()

    def greet(i, _):
        other = lax.rem(mine_id + i, n_dev)
        pl.semaphore_signal(
            barrier, inc=1, device_id={"seq": other // n_exp, "exp": lax.rem(other, n_exp)}
        )
        return 0

    with scope("greet"):
        lax.fori_loop(1, n_dev, greet, 0)

    with scope("prep"):
        hit = jnp.zeros((1, row_count), F32)
        for i in range(ids_ref.shape[0]):
            hit = jnp.maximum(hit, jnp.where(ids_ref[i : i + 1, :] == z, 1.0, 0.0))
        row_id = lax.broadcasted_iota(jnp.int32, (row_count, row_count), 0)
        col_id = lax.broadcasted_iota(jnp.int32, (row_count, row_count), 1)
        same = jnp.logical_and(row_id // tok == col_id // tok, row_id < col_id)
        before = dot(
            jnp.broadcast_to(hit, (16, row_count)).astype(BF), jnp.where(same, 1.0, 0.0).astype(BF)
        )
        rank = before[0:1].astype(jnp.int32)
        group = lax.broadcasted_iota(jnp.int32, (1, row_count), 1) // tok
        place = jnp.where(hit > 0.5, rank, -1)
        slots = lax.broadcasted_iota(jnp.int32, (main, tok), 0)
        for g in range(n_exp):
            chosen = slots == place[:, g * tok : (g + 1) * tok]
            pick[g] = jnp.where(chosen, 1.0, 0.0).astype(BF)
        over = jnp.where(place >= main, (place - main) * n_exp + group, -1)
        chosen = lax.broadcasted_iota(jnp.int32, (16, row_count), 0) == over
        pick_tail[...] = jnp.where(chosen, 1.0, 0.0).astype(BF)

    with scope("barrier"):
        pl.semaphore_wait(barrier, n_dev - 1)

    def z_copy(side, k, d, owner, target):
        return pltpu.make_async_remote_copy(
            src_ref=gath.at[k, owner],
            dst_ref=gath.at[k, owner],
            send_sem=zs_sem.at[side, k, d],
            recv_sem=zr_sem.at[side, k, d],
            device_id={"exp": target},
        )

    def z_send(k, d):
        @pl.when(jnp.logical_and(z < n_exp - 1, z - d >= 0))
        def _():
            z_copy(0, k, d, z - d, z + 1).start()

        @pl.when(jnp.logical_and(z > 0, z + d < n_exp))
        def _():
            z_copy(1, k, d, z + d, z - 1).start()

    def z_sent(k, d):
        @pl.when(jnp.logical_and(z < n_exp - 1, z - d >= 0))
        def _():
            z_copy(0, k, d, z - d, z + 1).wait_send()

        @pl.when(jnp.logical_and(z > 0, z + d < n_exp))
        def _():
            z_copy(1, k, d, z + d, z - 1).wait_send()

    def z_take(k, d):
        @pl.when(z - d >= 0)
        def _():
            z_copy(0, k, d - 1, z - d, z).wait_recv()

        @pl.when(z + d < n_exp)
        def _():
            z_copy(1, k, d - 1, z + d, z).wait_recv()

    with scope("own"):
        for k in range(parts):
            pltpu.make_async_copy(
                grad_hbm.at[:, pl.ds(k * width, width)], gath.at[k, z], load_sem.at[k]
            ).wait()
            z_send(k, 0)

    def bit_of(half, stage):
        if stage == n_stage:
            return 1
        return bits[stage] if half == 0 else bits[n_stage - 1 - stage]

    def x_copies(u, stage, here):
        masks = [()]
        for i in range(stage):
            masks = masks + [m + (i,) for m in masks]
        copies = []
        for j, mask in enumerate(masks):
            for half in range(2):
                owner = me
                for i in mask:
                    owner = flip(owner, bit_of(half, i))
                slot = (1 << stage) - 1 + j
                if not here:
                    owner = flip(owner, bit_of(half, stage))
                if u is None:
                    index, ref = 2 * units + half, tail.at[half, owner]
                else:
                    index, ref = 2 * u + half, rows.at[2 * u + half, owner]
                copies.append(pltpu.make_async_remote_copy(
                    src_ref=ref,
                    dst_ref=ref,
                    send_sem=xs_sem.at[index, slot],
                    recv_sem=xr_sem.at[index, slot],
                    device_id={"seq": flip(me, bit_of(half, stage))},
                ))
        return copies

    def x_start(u, stage):
        for mine in x_copies(u, stage, True):
            mine.start()

    def x_take(u, stage):
        for theirs in x_copies(u, stage, False):
            theirs.wait_recv()

    def x_pass(u, stage):
        x_take(u, stage - 1)
        x_start(u, stage)

    def x_sent(u):
        for stage in range(n_stage + 1):
            for mine in x_copies(u, stage, True):
                mine.wait_send()

    def d_copy(i):
        return pltpu.make_async_remote_copy(
            src_ref=span_sum.at[i],
            dst_ref=span_got.at[i],
            send_sem=ds_sem.at[i],
            recv_sem=dr_sem.at[i],
            device_id={"seq": flip(me, order[i])},
        )

    def settle():
        own = pl.multiple_of(z * tok, tok)
        named = [ids_ref[k : k + 1, pl.ds(own, tok)] for k in range(ids_ref.shape[0])]
        expert = lax.broadcasted_iota(jnp.int32, (16, tok), 0)
        member = jnp.zeros((16, tok), F32)
        for ids in named:
            member = jnp.maximum(member, jnp.where(ids == expert, 1.0, 0.0))
        earlier = lax.broadcasted_iota(jnp.int32, (tok, tok), 0) < lax.broadcasted_iota(
            jnp.int32, (tok, tok), 1
        )
        ranks = dot(member.astype(BF), jnp.where(earlier, 1.0, 0.0).astype(BF)).astype(jnp.int32)
        for k, ids in enumerate(named):
            slot = jnp.zeros((1, tok), jnp.int32)
            shift = jnp.zeros((1, tok), jnp.int32)
            for e in range(n_exp):
                slot += jnp.where(ids == e, ranks[e : e + 1], 0)
                shift += jnp.where(ids == e, (turn_of(e, z) % 2) * main, 0)
            far = (me // 2) * 16 + (slot - main) * 2 * n_exp + (me % 2) * n_exp + z
            spot[k : k + 1, :] = jnp.where(slot < main, shift + slot, far)
            spot[2 + k : 3 + k, :] = ids * 2 + jnp.where(slot < main, 0, 1)

    def prepare():
        row_id = lax.broadcasted_iota(jnp.int32, (row_count, row_count), 0)
        col_id = lax.broadcasted_iota(jnp.int32, (row_count, row_count), 1)
        tri = jnp.where(row_id <= col_id, 1.0, 0.0)
        cum = dot(decay_ref[...], tri, precision=highest)
        cum_ref[...] = cum
        cum_t[...] = jnp.transpose(cum)
        step_t[...] = jnp.transpose(step_ref[...])
        b_t[...] = jnp.transpose(b_ref[...])
        shape = (cum.shape[0], channels)
        own = lax.broadcasted_iota(jnp.int32, shape, 1) // HEAD == lax.broadcasted_iota(
            jnp.int32, shape, 0
        )
        end = jnp.sum(jnp.where(own, cum[:, row_count - 1 :], 0.0), axis=0, keepdims=True)
        span_sum[0] = jnp.broadcast_to(end, (8, channels))
        keep = lax.broadcasted_iota(jnp.int32, (block, block), 1) >= lax.broadcasted_iota(
            jnp.int32, (block, block), 0
        )
        for i in range(blocks):
            span = slice(i * block, (i + 1) * block)
            cross = dot(b_t[span, :], c_ref[:, span], precision=highest)
            bc[i] = jnp.where(keep, cross, 0.0)
        acc[...] = jnp.zeros_like(acc)
        acc_tail[...] = jnp.zeros_like(acc_tail)

    left_of = lax.broadcasted_iota(jnp.int32, (1, lane), 1) < HEAD
    perm_row = lax.broadcasted_iota(jnp.int32, (256, 256), 0)
    perm_col = lax.broadcasted_iota(jnp.int32, (256, 256), 1)

    def project(job):
        b, n = job // parts, job % parts
        q_first = pl.multiple_of((b % 2) * 16, 16)
        c_first = (b // 2) * 32

        @pl.when(n == 0)
        def _():
            swap = jnp.where(perm_col == (perm_row % 16) * 16 + perm_row // 16, 1.0, 0.0).astype(BF)
            for i in range(2):
                saved = hid[pl.ds(c_first + 16 * i, 16), pl.ds(q_first, 16), :]
                saved = saved.reshape(256, hid.shape[2])
                turned[256 * i : 256 * (i + 1), :] = dot(swap, saved).astype(BF)

        part = dot(turned[...], down[n])
        for i in range(2):
            y_ref[n, pl.ds(q_first, 16), pl.ds(pl.multiple_of(c_first + 16 * i, 16), 16), :] = part[
                256 * i : 256 * (i + 1)
            ].reshape(16, 16, width)

    def hoist(j):
        span = pl.ds(pl.multiple_of(j * lane, lane), lane)
        cols = [column(cum_t[...], 2 * j + i) for i in range(2)]
        rowv = [cum_ref[pl.ds(2 * j + i, 1), :] for i in range(2)]
        steps = [column(step_t[...], 2 * j + i) for i in range(2)]
        steps_col = jnp.where(left_of, steps[0], steps[1])
        col = jnp.where(left_of, cols[0], cols[1])
        end_row = jnp.where(left_of, cols[0][row_count - 1 :], cols[1][row_count - 1 :])
        fac[:, span] = steps_col * jnp.exp(end_row - col)
        for i in range(blocks):
            lo, hi = i * block, (i + 1) * block
            if i < blocks - 1:
                fac_mid[lo:hi, span] = steps_col[lo:hi] * jnp.exp(col[hi - 1 : hi] - col[lo:hi])
            for q in range(2):
                r = rowv[q][:, lo:hi]
                w = jnp.exp(jnp.minimum(r - cols[q][lo:hi], 0.0)) * (bc[i] * steps[q][lo:hi])
                w_top, w_low = halves(w)
                mix[j, i, q * block : (q + 1) * block, :] = w_top
                mix[j, i, (2 + q) * block : (3 + q) * block, :] = w_low
                base = rowv[q][:, lo - 1 : lo] if i else jnp.zeros((1, 1), F32)
                m_top, m_low = halves(c_ref[:, lo:hi] * jnp.exp(r - base))
                lead[j, i, q * n_state : (q + 1) * n_state, :] = m_top
                lead[j, i, (2 + q) * n_state : (3 + q) * n_state, :] = m_low

    def state_step(j, _):
        span = pl.ds(pl.multiple_of(j * lane, lane), lane)
        rowv = [cum_ref[pl.ds(2 * j + q, 1), :] for q in range(2)]
        ends = [[r[:, hi - 1 : hi] for r in rowv] for hi in range(block, row_count + 1, block)]
        state = jnp.zeros((n_state, lane), F32)
        for i in reversed(range(blocks)):
            g_top, g_low = halves(inner[i * block : (i + 1) * block, span])
            x = dot(lead[j, i], jnp.concatenate([g_top, g_low], axis=1))
            x = x[:, :lane] + jnp.concatenate(
                [x[: 2 * n_state, lane:], jnp.zeros((2 * n_state, lane), F32)], axis=0
            )
            x = x[: 2 * n_state] + x[2 * n_state :]
            if i < blocks - 1:
                mid[i, :, span] = state
            edge = jnp.where(left_of, ends[i][0], ends[i][1])
            if i:
                edge = edge - jnp.where(left_of, ends[i - 1][0], ends[i - 1][1])
            state = jnp.where(left_of, x[:n_state], x[n_state:]) + jnp.exp(edge) * state
        agg[0, :, span] = state
        return 0

    def within_step(j, _):
        span = pl.ds(pl.multiple_of(j * lane, lane), lane)
        skip = skip_ref[:, span]
        for i in range(blocks):
            lo, hi = i * block, (i + 1) * block
            g = inner[lo:hi, span]
            g_top, g_low = halves(g)
            x = dot(mix[j, i], jnp.concatenate([g_top, g_low], axis=1))
            part = []
            for q in range(2):
                top = x[q * block : (q + 1) * block]
                low = x[(2 + q) * block : (3 + q) * block]
                part.append(top[:, :lane] + top[:, lane:] + low[:, :lane])
            result = jnp.where(left_of, part[0], part[1]) + skip * g
            if i < blocks - 1:
                seen = dot(b_t[lo:hi, :], mid[i, :, span], precision=highest)
                result += fac_mid[lo:hi, span] * seen
            inner[lo:hi, span] = result
        return 0

    def scores(u):
        i, c = u // parts, u % parts
        g = nearest(z, i)

        def one(s, _):
            total = acc[s, i]
            for half in range(2):
                part = rows[2 * u + half, s].astype(F32) * y_ref[
                    c, s * n_exp + g, :, half * half_w : (half + 1) * half_w
                ]
                for j in range(half_w // 128):
                    total = total + part[:, j * 128 : (j + 1) * 128]
            acc[s, i] = total
            return 0

        lax.fori_loop(0, n_seq, one, 0)

    low_half = lax.broadcasted_iota(jnp.int32, (2 * n_exp, width), 0) < n_exp

    def tail_scores():
        def one(p, _):
            sums = [acc_tail[p, i] for i in range(extra)]
            for c in range(parts):
                half, at = c // 2, (c % 2) * width
                first = tail[half, 2 * p].astype(F32)[: 2 * n_exp, at : at + width]
                second = tail[half, 2 * p + 1].astype(F32)[: 2 * n_exp, at : at + width]
                even = jnp.where(low_half, first, pltpu.roll(second, n_exp, 0))
                odd = jnp.where(low_half, pltpu.roll(first, n_exp, 0), second)
                for i, part in enumerate((even, odd)):
                    first_q = pl.multiple_of(p * 2 * n_exp, 2 * n_exp)
                    part = part * y_tail[c, i, pl.ds(first_q, 2 * n_exp), :]
                    for j in range(width // 128):
                        sums[i] = sums[i] + part[:, j * 128 : (j + 1) * 128]
            for i in range(extra):
                acc_tail[p, i] = sums[i]
            return 0

        lax.fori_loop(0, n_seq // 2, one, 0)

    def unit_step(t, _):
        i, c = t // parts, t % parts

        with scope("ztake"):
            @pl.when(i >= 1)
            def _():
                z_take(c, i)

            @pl.when(jnp.logical_and(i >= 1, i < n_exp - 1))
            def _():
                z_send(c, i)

        g = nearest(z, i)
        with scope("pick"):
            taken = dot(pick[g], gath[c, g]).astype(BF)
            rows[2 * t, me] = taken[:, :half_w]
            rows[2 * t + 1, me] = taken[:, half_w:]
            x_start(t, 0)

        with scope("xpass1"):
            @pl.when(t >= LAG_FIRST)
            def _():
                x_pass(t - LAG_FIRST, 1)

        with scope("xpass2"):
            @pl.when(t >= LAG_SECOND)
            def _():
                x_pass(t - LAG_SECOND, 2)

        with scope("once"):
            @pl.when(t == 0)
            def _():
                prepare()
                d_copy(0).start()
                settle()
                hid_copy.wait()

            for k in range(parts):
                @pl.when(t == k)
                def _(k=k):
                    pltpu.make_async_copy(
                        down_hbm.at[0, :, pl.ds(k * width, width)], down.at[k], down_sem.at[k]
                    ).wait()
                    pltpu.make_async_copy(
                        proj_hbm.at[:, pl.ds(k * width, width)], proj.at[k], proj_sem.at[k]
                    ).wait()

            for i_ in range(len(order)):
                @pl.when(t == 2 * i_ + 3)
                def _(i_=i_):
                    d_copy(i_).wait_recv()
                    if i_ + 1 < len(order):
                        span_sum[i_ + 1] = span_sum[i_] + span_got[i_]
                        d_copy(i_ + 1).start()

        with scope("project"):
            @pl.when(jnp.logical_and(t >= parts - 1, t < 3 * parts - 1))
            def _():
                project(2 * (t - parts + 1))
                project(2 * (t - parts + 1) + 1)

            @pl.when(jnp.logical_and(t >= 2 * parts, t < 3 * parts))
            def _():
                saved = hid[main:cap].reshape(extra * hid.shape[1], hid.shape[2])
                y_tail[c] = dot(saved, down[c]).reshape(extra, hid.shape[1], width)

        with scope("inner"):
            @pl.when(i % 2 == 1)
            def _():
                other = nearest(z, i - 1)
                both = jnp.concatenate([gath[c, other], gath[c, g]], axis=0)
                part = dot(both, proj[c], ((1,), (1,)))
                first = pl.ds(pl.multiple_of(other * tok, tok), tok)
                second = pl.ds(pl.multiple_of(g * tok, tok), tok)

                @pl.when(c == 0)
                def _():
                    inner[first, :] = part[:tok]
                    inner[second, :] = part[tok:]

                @pl.when(c > 0)
                def _():
                    inner[first, :] += part[:tok]
                    inner[second, :] += part[tok:]

        with scope("hoist"):
            @pl.when(jnp.logical_and(t >= units - pairs, t < units))
            def _():
                hoist(t - (units - pairs))

        with scope("tailrows"):
            @pl.when(i == n_exp - 1)
            def _():
                left = dot(pick_tail[...], gath[c].reshape(row_count, width)).astype(BF)
                tail[c // 2, me, :, pl.ds(pl.multiple_of((c % 2) * width, width), width)] = left

        with scope("score"):
            @pl.when(t >= 3 * parts)
            def _():
                for v in range(2):
                    u = 2 * (t - 3 * parts) + v
                    x_take(u, n_stage)
                    scores(u)

        return 0

    with scope("unitloop"):
        lax.fori_loop(0, units, unit_step, 0)

    def a_copy(i):
        return pltpu.make_async_remote_copy(
            src_ref=agg.at[i],
            dst_ref=got.at[i],
            send_sem=as_sem.at[i],
            recv_sem=ar_sem.at[i],
            device_id={"seq": flip(me, order[i])},
        )

    reach = [jnp.zeros((1, channels), F32)]

    def combine(i):
        a_copy(i).wait_recv()
        low = ((me // order[i]) % 2) == 0
        other, other_t = got[i], span_got[i, 0:1, :]
        own, own_t = agg[i], span_sum[i, 0:1, :]
        added = jnp.where(low, jnp.exp(reach[0]) * other, 0.0)
        if i == 0:
            carry[...] = added
        else:
            carry[...] += added
        reach[0] = reach[0] + jnp.where(low, other_t, 0.0)
        if i + 1 < len(order):
            first = jnp.where(low, own, other)
            first_t = jnp.where(low, own_t, other_t)
            second = jnp.where(low, other, own)
            agg[i + 1] = first + jnp.exp(first_t) * second
            a_copy(i + 1).start()

    def mail_copy(other, source, slot):
        return pltpu.make_async_remote_copy(
            src_ref=mail.at[other // n_exp, turn_of(z, lax.rem(other, n_exp)) // 2],
            dst_ref=inbox.at[source],
            send_sem=ms_sem.at[slot],
            recv_sem=mr_sem.at[source],
            device_id={"seq": other // n_exp, "exp": lax.rem(other, n_exp)},
        )

    def post(i, _):
        other = lax.rem(mine_id + i, n_dev)
        mail_copy(other, mine_id, other).start()
        return 0

    def take(i, _):
        other = lax.rem(mine_id + i, n_dev)
        mail_copy(other, other, other).wait_recv()
        return 0

    def posted(i, _):
        other = lax.rem(mine_id + i, n_dev)
        mail_copy(other, mine_id, other).wait_send()
        return 0

    done = [2 * parts]

    def pace(stage):
        with scope("p%d" % stage):
            if stage == 0:
                x_start(None, 0)
                x_pass(units - 2, 1)
            if stage == 1:
                x_pass(units - 4, 2)
                x_pass(units - 1, 1)
                x_pass(None, 1)
            if stage == 2:
                x_pass(units - 3, 2)
            if stage == 3:
                x_pass(units - 2, 2)
            if stage == 4:
                x_pass(units - 1, 2)
                x_pass(None, 2)

    def count(upto):
        with scope("c%d" % upto):
            for u in range(done[0], upto):
                x_take(u, n_stage)
                scores(u)
            done[0] = max(done[0], upto)

    pace(0)
    with scope("state"):
        lax.fori_loop(0, pairs, state_step, 0)
        a_copy(0).start()
    pace(1)
    with scope("within1"):
        lax.fori_loop(0, pairs // 4, within_step, 0)
    pace(2)
    with scope("comb0"):
        combine(0)
    count(units - 4)
    pace(3)
    with scope("within2"):
        lax.fori_loop(pairs // 4, pairs // 2, within_step, 0)
    pace(4)
    with scope("comb1"):
        combine(1)
    count(units)
    with scope("tailscore"):
        x_take(None, n_stage)
        tail_scores()

    with scope("finish"):
        wide = jnp.transpose(acc_tail[...].reshape(n_seq // 2 * extra * 2 * n_exp, 128))
        wide = jnp.sum(wide, axis=0, keepdims=True)
        wide = jnp.concatenate([wide, jnp.zeros((1, 128 - wide.shape[1]), F32)], axis=1)

        def finish(s, _):
            for i in range(n_exp // 2):
                both = jnp.transpose(acc[s, 2 * i : 2 * i + 2].reshape(2 * main, 128))
                mail[s, i, 0:1, :] = jnp.sum(both, axis=0, keepdims=True)
                mail[s, i, 1:2, :] = wide
            return 0

        lax.fori_loop(0, n_seq, finish, 0)
    with scope("post"):
        lax.fori_loop(1, n_dev, post, 0)
        inbox[mine_id] = mail[me, 0]

    with scope("within3"):
        lax.fori_loop(pairs // 2, pairs, within_step, 0)
    with scope("comb2"):
        combine(2)
    with scope("out"):
        for i in range(blocks):
            lo, hi = i * block, (i + 1) * block
            from_carry = dot(b_t[lo:hi, :], carry[...], precision=highest)
            out_ref[lo:hi, :] = (inner[lo:hi, :] + fac[lo:hi, :] * from_carry).astype(BF)

    with scope("drain"):
        def x_drain(u, _):
            x_sent(u)
            return 0

        lax.fori_loop(0, units, x_drain, 0)
        x_sent(None)
        for k in range(parts):
            for d in range(n_exp - 1):
                z_sent(k, d)
        for i in range(len(order)):
            a_copy(i).wait_send()
            d_copy(i).wait_send()
    with scope("mail"):
        lax.fori_loop(1, n_dev, take, 0)
    with scope("gate"):
        for e in range(n_exp):
            total = inbox[e]
            for i in range(1, n_seq):
                total = total + inbox[i * n_exp + e]
            vals[2 * e : 2 * e + 2, :] = total
        for k in range(ids_ref.shape[0]):
            at = lax.broadcasted_iota(jnp.int32, (128, tok), 0) == spot[k : k + 1, :]
            found = dot(vals[...], jnp.where(at, 1.0, 0.0), precision=highest)
            pickd = lax.broadcasted_iota(jnp.int32, (2 * n_exp, tok), 0) == spot[2 + k : 3 + k, :]
            gate_ref[k : k + 1, :] = jnp.sum(jnp.where(pickd, found, 0.0), axis=0, keepdims=True)
        lax.fori_loop(1, n_dev, posted, 0)


def plan(n_seq, n_exp, tok, depth, channels, cap, hidden, state, top):
    parts = 4
    width = depth // parts
    main = cap // 16 * 16
    extra = cap - main
    row_count = n_exp * tok
    block = min(256, row_count)
    blocks = row_count // block
    heads = channels // HEAD
    pairs = heads // 2
    stages = n_seq.bit_length() - 1
    steps = n_exp - 1
    units = n_exp * parts
    groups = n_seq * n_exp
    shapes = [
        ((parts, n_exp, tok, width), BF),
        ((parts, channels, width), BF),
        ((cap, groups, hidden), BF),
        ((parts, hidden, width), BF),
        ((512, hidden), BF),
        ((parts, groups, main, width), F32),
        ((parts, extra, groups, width), F32),
        ((2 * units, n_seq, main, width // 2), BF),
        ((2, n_seq, 16, depth // 2), BF),
        ((n_exp, main, tok), BF),
        ((16, row_count), BF),
        ((row_count, channels), F32),
        ((row_count, channels), F32),
        ((max(row_count - block, 8), channels), F32),
        ((n_seq, n_exp, main, 128), F32),
        ((n_seq // 2, extra, 2 * n_exp, 128), F32),
        ((heads, row_count), F32),
        ((row_count, heads), F32),
        ((row_count, heads), F32),
        ((row_count, state), F32),
        ((blocks, block, block), F32),
        ((pairs, blocks, 4 * block, block), BF),
        ((pairs, blocks, 4 * state, block), BF),
        ((max(blocks - 1, 1), state, channels), F32),
        ((stages, 8, channels), F32),
        ((stages, 8, channels), F32),
        ((stages, state, channels), F32),
        ((stages, state, channels), F32),
        ((state, channels), F32),
        ((8, tok), jnp.int32),
        ((n_seq, n_exp // 2, 2, 128), F32),
        ((groups, 2, 128), F32),
        ((2 * n_exp, 128), F32),
    ]
    total = 0
    for shape, kind in shapes:
        size = 1
        for extent in shape:
            size *= extent
        total += size * (2 if kind is BF else 4)
    fits = (
        total < VMEM_ROOM - (4 << 20)
        and n_seq & (n_seq - 1) == 0
        and stages == 3
        and n_exp == 4
        and groups == 32
        and main == 64
        and extra == 2
        and top == 2
        and depth % (256 * parts) == 0
        and channels % (2 * HEAD) == 0
        and pairs <= units // 2
        and row_count % block == 0
        and tok == 128
    )
    sems = [
        (parts,), (), (parts,), (parts,),
        (2, parts, steps), (2, parts, steps),
        (2 * units + 2, n_seq - 1), (2 * units + 2, n_seq - 1),
        (stages,), (stages,), (stages,), (stages,),
        (groups,), (groups,),
    ]
    return fits, (n_seq, n_exp, tok, cap, parts, width), shapes, sems


def quick(
    fitted, grad_out, out_proj, step_size, log_decay, b_input, c_output, skip_gain, expert_ids,
    hidden_act, w_down,
):
    _, sizes, shapes, sems = fitted
    n_seq, n_exp, tok, cap, parts, width = sizes
    vmem = pl.BlockSpec(memory_space=pltpu.VMEM)
    hbm = pl.BlockSpec(memory_space=pl.ANY)
    row_count, channels = n_exp * tok, out_proj.shape[0]
    return pl.pallas_call(
        functools.partial(fused, sizes),
        out_shape=(
            jax.ShapeDtypeStruct((row_count, channels), BF),
            jax.ShapeDtypeStruct((expert_ids.shape[1], tok), F32),
        ),
        in_specs=[hbm] * 4 + [vmem] * 6,
        out_specs=(vmem, vmem),
        scratch_shapes=[pltpu.VMEM(shape, kind) for shape, kind in shapes]
        + [pltpu.SemaphoreType.DMA(s) if s else pltpu.SemaphoreType.DMA for s in sems],
        compiler_params=pltpu.CompilerParams(
            collective_id=0, has_side_effects=True, vmem_limit_bytes=VMEM_ROOM
        ),
    )(
        grad_out, out_proj, hidden_act.transpose(0, 2, 1, 3), w_down, step_size, log_decay, b_input, c_output,
        skip_gain.reshape(1, -1), expert_ids.T,
    )


def route(*args):
    grad_out, out_proj, step_size, log_decay, b_input, c_output, skip_gain, ids, hidden, down = args
    fitted = plan(
        lax.axis_size("seq"), lax.axis_size("exp"), grad_out.shape[0], grad_out.shape[1],
        out_proj.shape[0], hidden.shape[2], hidden.shape[3], b_input.shape[0], ids.shape[1],
    )
    if fitted[0]:
        return quick(fitted, *args)
    return shards(*args)


def solution(mesh):
    in_specs = (
        P(("seq", "exp"), None),
        P("exp", None),
        P("exp", "seq"),
        P("exp", "seq"),
        P(None, "seq"),
        P(None, "seq"),
        P("exp"),
        P("seq", None),
        P("exp", None, None, "seq"),
        P("exp", "seq", None),
    )
    out_specs = (P("seq", "exp"), P(None, ("seq", "exp")))
    return jax.shard_map(route, mesh=mesh, in_specs=in_specs, out_specs=out_specs, check_vma=False)
```

time: 108 us -> 72.1 us (0.67)
  Pallas kernels: 101 us -> 67.7 us
  other arithmetic: 2.59 us -> 0 us
    pallas_call x1, Pallas kernels: 101 us -> 67.7 us  [quick(): pl.pallas_call(functools.partial(fused, sizes), out_shape=(jax.ShapeDtype...]
    unnamed x1 -> x2, local copies, waits for them, and re-layouts: 2.26 us -> 3.5 us
where the time goes in v1:
time: 72.1 us; the launch traced here: 71.8 us
  Pallas kernels  67.7 us (94%)
  local copies, waits for them, and re-layouts  3.5 us (5%)
    pallas_call x1, Pallas kernels, quick(): pl.pallas_call(functools.partial(fused, sizes), out_shape=(jax.ShapeDtype...  67.7 us
    unnamed x2, local copies, waits for them, and re-layouts  3.5 us

profile of v1, /device:TPU:0, one launch (start us, length us, event | category | flops | bytes accessed | tf_op | source)
XLA Modules:
  0.0 71.8 jit_solution(8602240381121431622)
XLA Ops:
  0.6 67.7 %shard_map.113 = (bf16[512,1024]{1,0:T(8,128)(2,1)}, f32[2,128]{1,0:T(2,128)}) custom-call(bf16[128,2048]{1,0:T(8,128)(2,1)} %grad_hbm.1, bf16[1024,2048]{1,0:T(8,128)(2,1)} %proj_hbm.1, bf16[1,66,32,1024]{3,2,1,0:T(8,128)(2,1)} %bitcast.3, bf16[1,1024,2048]{2,1,0:T(8,128)(2,1)} %down_hbm.1, f32[16,512]{1,0:T(8,128)} %step_ref.1, f32[16,512]{1,0:T(8,128)} %decay_ref.1, ...), custom_call_target="tpu_custom_call" | custom-call | tf_op jit(solution)/shard_map/pallas_call | solution.py:913
  68.3 2.3 %copy.14 = bf16[512,1024]{1,0:T(8,128)(2,1)} copy(bf16[512,1024]{1,0:T(8,128)(2,1)} %get-tuple-element.4) | data formatting | bytes 2097152
  70.6 1.2 %copy.15 = f32[2,128]{1,0:T(2,128)} copy(f32[2,128]{1,0:T(2,128)} %get-tuple-element.5) | data formatting | bytes 2048

commit v2 on v1

--- a/solution.py
+++ b/solution.py
@@ -164,8 +164,16 @@
 VMEM_ROOM = 63 << 20
 BF = jnp.bfloat16
 F32 = jnp.float32
-LAG_FIRST = 2
-LAG_SECOND = 4
+LAG_FIRST = 1
+LAG_SECOND = 3
+FIRST_STEPS = {
+    0: ((0, 1),),
+    1: ((1, 1), (2, 1)),
+    2: ((3, 1), (0, 2)),
+    3: ((1, 2),),
+    4: ((2, 2),),
+    5: ((3, 2),),
+}
 scope = jax.named_scope
 
 
@@ -203,13 +211,13 @@
 
 def fused(
     sizes,
-    grad_hbm, proj_hbm, hid_hbm, down_hbm, step_ref, decay_ref, b_ref, c_ref, skip_ref, ids_ref,
-    out_ref, gate_ref,
+    grad_hbm, proj_hbm, hid_hbm, down_hbm, step_hbm, decay_hbm, b_hbm, c_hbm, skip_hbm, ids_hbm,
+    out_hbm, gate_ref,
     gath, proj, hid, down, turned, y_ref, y_tail, rows, tail, pick, pick_tail, inner, fac, fac_mid,
     acc, acc_tail, cum_ref, cum_t, step_t, b_t, bc, mix, lead, mid, span_sum, span_got, agg, got,
-    carry, spot, mail, inbox, vals,
-    load_sem, hid_sem, down_sem, proj_sem,
-    zs_sem, zr_sem, xs_sem, xr_sem, ds_sem, dr_sem, as_sem, ar_sem, ms_sem, mr_sem,
+    carry, spot, mail, inbox, vals, out_buf, where_at, step_ref, decay_ref, b_ref, c_ref, skip_ref, ids_ref, b_wide,
+    load_sem,
+    zs_sem, zr_sem, xs_sem, xr_sem, ds_sem, dr_sem, as_sem, ar_sem, ms_sem, mr_sem, out_sem,
 ):
     n_seq, n_exp, tok, cap, parts, width = sizes
     me = lax.axis_index("seq")
@@ -231,34 +239,51 @@
     units = n_exp * parts
     n_state = b_t.shape[1]
 
-    for k in range(parts):
-        pltpu.make_async_copy(
-            grad_hbm.at[:, pl.ds(k * width, width)], gath.at[k, z], load_sem.at[k]
-        ).start()
-    hid_copy = pltpu.make_async_copy(hid_hbm.at[0], hid, hid_sem)
-    hid_copy.start()
-    for k in range(parts):
-        pltpu.make_async_copy(
-            down_hbm.at[0, :, pl.ds(k * width, width)], down.at[k], down_sem.at[k]
-        ).start()
-    for k in range(parts):
-        pltpu.make_async_copy(
-            proj_hbm.at[:, pl.ds(k * width, width)], proj.at[k], proj_sem.at[k]
-        ).start()
-
+    def load(k):
+        return pltpu.make_async_copy(
+            grad_hbm.at[:, pl.ds(k * width, width)], gath.at[k, z], load_sem.at[0]
+        )
+
+    def down_load(k):
+        return pltpu.make_async_copy(
+            down_hbm.at[0, :, pl.ds(k * width, width)], down.at[k], load_sem.at[1]
+        )
+
+    def proj_load(k):
+        return pltpu.make_async_copy(
+            proj_hbm.at[:, pl.ds(k * width, width)], proj.at[k], load_sem.at[2]
+        )
+
+    hid_copy = pltpu.make_async_copy(hid_hbm.at[0], hid, load_sem.at[3])
+    ids_copy = pltpu.make_async_copy(ids_hbm, ids_ref, load_sem.at[4])
+    small = [
+        pltpu.make_async_copy(src, dst, load_sem.at[5 + i])
+        for i, (src, dst) in enumerate((
+            (step_hbm, step_ref), (decay_hbm, decay_ref), (b_hbm, b_ref), (c_hbm, c_ref),
+            (skip_hbm, skip_ref),
+        ))
+    ]
     barrier = pltpu.get_barrier_semaphore()
 
-    def greet(i, _):
-        other = lax.rem(mine_id + i, n_dev)
-        pl.semaphore_signal(
-            barrier, inc=1, device_id={"seq": other // n_exp, "exp": lax.rem(other, n_exp)}
-        )
-        return 0
-
     with scope("greet"):
-        lax.fori_loop(1, n_dev, greet, 0)
+        for bit in order:
+            pl.semaphore_signal(barrier, inc=1, device_id={"seq": flip(me, bit)})
+
+        @pl.when(z > 0)
+        def _():
+            pl.semaphore_signal(barrier, inc=1, device_id={"exp": z - 1})
+
+        @pl.when(z < n_exp - 1)
+        def _():
+            pl.semaphore_signal(barrier, inc=1, device_id={"exp": z + 1})
 
     with scope("prep"):
+        for k in range(parts):
+            load(k).start()
+        ids_copy.start()
+        for copy in small:
+            copy.start()
+        ids_copy.wait()
         hit = jnp.zeros((1, row_count), F32)
         for i in range(ids_ref.shape[0]):
             hit = jnp.maximum(hit, jnp.where(ids_ref[i : i + 1, :] == z, 1.0, 0.0))
@@ -280,13 +305,14 @@
         pick_tail[...] = jnp.where(chosen, 1.0, 0.0).astype(BF)
 
     with scope("barrier"):
-        pl.semaphore_wait(barrier, n_dev - 1)
+        sides = jnp.minimum(z, 1) + jnp.minimum(n_exp - 1 - z, 1)
+        pl.semaphore_wait(barrier, len(order) + sides)
 
     def z_copy(side, k, d, owner, target):
         return pltpu.make_async_remote_copy(
             src_ref=gath.at[k, owner],
             dst_ref=gath.at[k, owner],
-            send_sem=zs_sem.at[side, k, d],
+            send_sem=zs_sem.at[side, d],
             recv_sem=zr_sem.at[side, k, d],
             device_id={"exp": target},
         )
@@ -300,14 +326,17 @@
         def _():
             z_copy(1, k, d, z + d, z - 1).start()
 
-    def z_sent(k, d):
+    def settled(ref, sem):
+        pltpu.make_async_copy(ref, ref, sem).wait()
+
+    def z_sent(d):
         @pl.when(jnp.logical_and(z < n_exp - 1, z - d >= 0))
         def _():
-            z_copy(0, k, d, z - d, z + 1).wait_send()
+            settled(gath.at[:, z], zs_sem.at[0, d])
 
         @pl.when(jnp.logical_and(z > 0, z + d < n_exp))
         def _():
-            z_copy(1, k, d, z + d, z - 1).wait_send()
+            settled(gath.at[:, z], zs_sem.at[1, d])
 
     def z_take(k, d):
         @pl.when(z - d >= 0)
@@ -319,10 +348,8 @@
             z_copy(1, k, d - 1, z + d, z).wait_recv()
 
     with scope("own"):
+        settled(gath.at[:, z], load_sem.at[0])
         for k in range(parts):
-            pltpu.make_async_copy(
-                grad_hbm.at[:, pl.ds(k * width, width)], gath.at[k, z], load_sem.at[k]
-            ).wait()
             z_send(k, 0)
 
     def bit_of(half, stage):
@@ -330,54 +357,54 @@
             return 1
         return bits[stage] if half == 0 else bits[n_stage - 1 - stage]
 
-    def x_copies(u, stage, here):
-        masks = [()]
+    def owners(half, stage):
+        held = [me]
         for i in range(stage):
-            masks = masks + [m + (i,) for m in masks]
-        copies = []
-        for j, mask in enumerate(masks):
+            held = held + [flip(owner, bit_of(half, i)) for owner in held]
+        return held
+
+    def x_start(u, stage):
+        for j in range(1 << stage):
             for half in range(2):
-                owner = me
-                for i in mask:
-                    owner = flip(owner, bit_of(half, i))
-                slot = (1 << stage) - 1 + j
-                if not here:
-                    owner = flip(owner, bit_of(half, stage))
-                if u is None:
-                    index, ref = 2 * units + half, tail.at[half, owner]
-                else:
-                    index, ref = 2 * u + half, rows.at[2 * u + half, owner]
-                copies.append(pltpu.make_async_remote_copy(
+                ref = rows.at[2 * u + half, owners(half, stage)[j]]
+                pltpu.make_async_remote_copy(
                     src_ref=ref,
                     dst_ref=ref,
-                    send_sem=xs_sem.at[index, slot],
-                    recv_sem=xr_sem.at[index, slot],
+                    send_sem=xs_sem.at[0],
+                    recv_sem=xr_sem.at[u, stage],
                     device_id={"seq": flip(me, bit_of(half, stage))},
-                ))
-        return copies
-
-    def x_start(u, stage):
-        for mine in x_copies(u, stage, True):
-            mine.start()
+                ).start()
 
     def x_take(u, stage):
-        for theirs in x_copies(u, stage, False):
-            theirs.wait_recv()
+        settled(rows.at[pl.ds(2 * u, 2), pl.ds(0, 1 << stage)], xr_sem.at[u, stage])
 
     def x_pass(u, stage):
         x_take(u, stage - 1)
         x_start(u, stage)
 
-    def x_sent(u):
-        for stage in range(n_stage + 1):
-            for mine in x_copies(u, stage, True):
-                mine.wait_send()
+    def t_start(half, stage):
+        for owner in owners(half, stage):
+            ref = tail.at[half, owner]
+            pltpu.make_async_remote_copy(
+                src_ref=ref,
+                dst_ref=ref,
+                send_sem=xs_sem.at[1],
+                recv_sem=xr_sem.at[units + half, stage],
+                device_id={"seq": flip(me, bit_of(half, stage))},
+            ).start()
+
+    def t_take(half, stage):
+        settled(tail.at[half, pl.ds(0, 1 << stage)], xr_sem.at[units + half, stage])
+
+    def t_pass(half, stage):
+        t_take(half, stage - 1)
+        t_start(half, stage)
 
     def d_copy(i):
         return pltpu.make_async_remote_copy(
             src_ref=span_sum.at[i],
             dst_ref=span_got.at[i],
-            send_sem=ds_sem.at[i],
+            send_sem=ds_sem,
             recv_sem=dr_sem.at[i],
             device_id={"seq": flip(me, order[i])},
         )
@@ -400,10 +427,15 @@
                 slot += jnp.where(ids == e, ranks[e : e + 1], 0)
                 shift += jnp.where(ids == e, (turn_of(e, z) % 2) * main, 0)
             far = (me // 2) * 16 + (slot - main) * 2 * n_exp + (me % 2) * n_exp + z
-            spot[k : k + 1, :] = jnp.where(slot < main, shift + slot, far)
-            spot[2 + k : 3 + k, :] = ids * 2 + jnp.where(slot < main, 0, 1)
+            at = lax.broadcasted_iota(jnp.int32, (128, tok), 0) == jnp.where(
+                slot < main, shift + slot, far
+            )
+            where_at[:, k * tok : (k + 1) * tok] = jnp.where(at, 1.0, 0.0).astype(BF)
+            spot[k : k + 1, :] = ids * 2 + jnp.where(slot < main, 0, 1)
 
     def prepare():
+        for copy in small:
+            copy.wait()
         row_id = lax.broadcasted_iota(jnp.int32, (row_count, row_count), 0)
         col_id = lax.broadcasted_iota(jnp.int32, (row_count, row_count), 1)
         tri = jnp.where(row_id <= col_id, 1.0, 0.0)
@@ -412,6 +444,8 @@
         cum_t[...] = jnp.transpose(cum)
         step_t[...] = jnp.transpose(step_ref[...])
         b_t[...] = jnp.transpose(b_ref[...])
+        b_top, b_low = halves(b_t[...])
+        b_wide[...] = jnp.concatenate([b_top, b_top, b_low], axis=1)
         shape = (cum.shape[0], channels)
         own = lax.broadcasted_iota(jnp.int32, shape, 1) // HEAD == lax.broadcasted_iota(
             jnp.int32, shape, 0
@@ -432,6 +466,8 @@
     perm_row = lax.broadcasted_iota(jnp.int32, (256, 256), 0)
     perm_col = lax.broadcasted_iota(jnp.int32, (256, 256), 1)
 
+    jobs = parts * main * hid.shape[1] // 512
+
     def project(job):
         b, n = job // parts, job % parts
         q_first = pl.multiple_of((b % 2) * 16, 16)
@@ -445,11 +481,26 @@
                 saved = saved.reshape(256, hid.shape[2])
                 turned[256 * i : 256 * (i + 1), :] = dot(swap, saved).astype(BF)
 
-        part = dot(turned[...], down[n])
-        for i in range(2):
-            y_ref[n, pl.ds(q_first, 16), pl.ds(pl.multiple_of(c_first + 16 * i, 16), 16), :] = part[
-                256 * i : 256 * (i + 1)
-            ].reshape(16, 16, width)
+            @pl.when(b == jobs // parts - 1)
+            def _():
+                turned[512:, :] = hid[main:cap].reshape(extra * hid.shape[1], hid.shape[2])
+
+        def keep_part(part):
+            for i in range(2):
+                c_from = pl.multiple_of(c_first + 16 * i, 16)
+                y_ref[n, pl.ds(q_first, 16), pl.ds(c_from, 16), :] = part[
+                    256 * i : 256 * (i + 1)
+                ].reshape(16, 16, width)
+
+        @pl.when(b < jobs // parts - 1)
+        def _():
+            keep_part(dot(turned[:512, :], down[n]))
+
+        @pl.when(b == jobs // parts - 1)
+        def _():
+            part = dot(turned[...], down[n])
+            keep_part(part)
+            y_tail[n] = part[512:].reshape(extra, hid.shape[1], width)
 
     def hoist(j):
         span = pl.ds(pl.multiple_of(j * lane, lane), lane)
@@ -496,6 +547,10 @@
         agg[0, :, span] = state
         return 0
 
+    def read_state(lo, hi, state):
+        top, low = halves(state)
+        return dot(b_wide[lo:hi, :], jnp.concatenate([top, low, top], axis=0))
+
     def within_step(j, _):
         span = pl.ds(pl.multiple_of(j * lane, lane), lane)
         skip = skip_ref[:, span]
@@ -511,7 +566,7 @@
                 part.append(top[:, :lane] + top[:, lane:] + low[:, :lane])
             result = jnp.where(left_of, part[0], part[1]) + skip * g
             if i < blocks - 1:
-                seen = dot(b_t[lo:hi, :], mid[i, :, span], precision=highest)
+                seen = read_state(lo, hi, mid[i, :, span])
                 result += fac_mid[lo:hi, span] * seen
             inner[lo:hi, span] = result
         return 0
@@ -539,9 +594,9 @@
         def one(p, _):
             sums = [acc_tail[p, i] for i in range(extra)]
             for c in range(parts):
-                half, at = c // 2, (c % 2) * width
-                first = tail[half, 2 * p].astype(F32)[: 2 * n_exp, at : at + width]
-                second = tail[half, 2 * p + 1].astype(F32)[: 2 * n_exp, at : at + width]
+                half, at = c // (parts // 2), (c % (parts // 2)) * width
+                first = tail[half, 2 * p].astype(F32)[:, at : at + width]
+                second = tail[half, 2 * p + 1].astype(F32)[:, at : at + width]
                 even = jnp.where(low_half, first, pltpu.roll(second, n_exp, 0))
                 odd = jnp.where(low_half, pltpu.roll(first, n_exp, 0), second)
                 for i, part in enumerate((even, odd)):
@@ -555,6 +610,24 @@
 
         lax.fori_loop(0, n_seq // 2, one, 0)
 
+    def choose(u, g, c):
+        taken = dot(pick[g], gath[c, g]).astype(BF)
+        rows[2 * u, me] = taken[:, :half_w]
+        rows[2 * u + 1, me] = taken[:, half_w:]
+        x_start(u, 0)
+
+    def first_step(c, _):
+        choose(c, z, c)
+        return 0
+
+    with scope("first"):
+        lax.fori_loop(0, parts, first_step, 0)
+        hid_copy.start()
+        for k in range(parts):
+            down_load(k).start()
+        for k in range(parts):
+            proj_load(k).start()
+
     def unit_step(t, _):
         i, c = t // parts, t % parts
 
@@ -567,22 +640,32 @@
             def _():
                 z_send(c, i)
 
-        g = nearest(z, i)
         with scope("pick"):
-            taken = dot(pick[g], gath[c, g]).astype(BF)
-            rows[2 * t, me] = taken[:, :half_w]
-            rows[2 * t + 1, me] = taken[:, half_w:]
-            x_start(t, 0)
-
-        with scope("xpass1"):
-            @pl.when(t >= LAG_FIRST)
-            def _():
-                x_pass(t - LAG_FIRST, 1)
-
-        with scope("xpass2"):
-            @pl.when(t >= LAG_SECOND)
-            def _():
-                x_pass(t - LAG_SECOND, 2)
+            @pl.when(i >= 1)
+            def _():
+                choose(t, nearest(z, i), c)
+
+        with scope("tailrows"):
+            @pl.when(i == n_exp - 1)
+            def _():
+                left = dot(pick_tail[...], gath[c].reshape(row_count, width))
+                at = pl.multiple_of((c % (parts // 2)) * width, width)
+                tail[c // (parts // 2), me, :, pl.ds(at, width)] = left[: 2 * n_exp].astype(BF)
+
+            for half in range(2):
+                @pl.when(t == units - 1 - (1 - half) * (parts // 2))
+                def _(half=half):
+                    t_start(half, 0)
+
+            @pl.when(t == units - 1)
+            def _():
+                t_pass(0, 1)
+
+        with scope("hoist0"):
+            @pl.when(jnp.logical_and(t >= 1, t <= 2))
+            def _():
+                for v in range(pairs // 4):
+                    hoist((t - 1) * (pairs // 4) + v)
 
         with scope("once"):
             @pl.when(t == 0)
@@ -590,17 +673,12 @@
                 prepare()
                 d_copy(0).start()
                 settle()
+
+            @pl.when(t == parts - 1)
+            def _():
                 hid_copy.wait()
-
-            for k in range(parts):
-                @pl.when(t == k)
-                def _(k=k):
-                    pltpu.make_async_copy(
-                        down_hbm.at[0, :, pl.ds(k * width, width)], down.at[k], down_sem.at[k]
-                    ).wait()
-                    pltpu.make_async_copy(
-                        proj_hbm.at[:, pl.ds(k * width, width)], proj.at[k], proj_sem.at[k]
-                    ).wait()
+                settled(down, load_sem.at[1])
+                settled(proj, load_sem.at[2])
 
             for i_ in range(len(order)):
                 @pl.when(t == 2 * i_ + 3)
@@ -616,48 +694,46 @@
                 project(2 * (t - parts + 1))
                 project(2 * (t - parts + 1) + 1)
 
-            @pl.when(jnp.logical_and(t >= 2 * parts, t < 3 * parts))
-            def _():
-                saved = hid[main:cap].reshape(extra * hid.shape[1], hid.shape[2])
-                y_tail[c] = dot(saved, down[c]).reshape(extra, hid.shape[1], width)
-
         with scope("inner"):
-            @pl.when(i % 2 == 1)
-            def _():
-                other = nearest(z, i - 1)
-                both = jnp.concatenate([gath[c, other], gath[c, g]], axis=0)
-                part = dot(both, proj[c], ((1,), (1,)))
-                first = pl.ds(pl.multiple_of(other * tok, tok), tok)
-                second = pl.ds(pl.multiple_of(g * tok, tok), tok)
+            @pl.when(i == n_exp - 1)
+            def _():
+                part = dot(gath[c].reshape(row_count, width), proj[c], ((1,), (1,)))
 
                 @pl.when(c == 0)
                 def _():
-                    inner[first, :] = part[:tok]
-                    inner[second, :] = part[tok:]
+                    inner[...] = part
 
                 @pl.when(c > 0)
                 def _():
-                    inner[first, :] += part[:tok]
-                    inner[second, :] += part[tok:]
+                    inner[...] += part
 
         with scope("hoist"):
-            @pl.when(jnp.logical_and(t >= units - pairs, t < units))
-            def _():
-                hoist(t - (units - pairs))
-
-        with scope("tailrows"):
-            @pl.when(i == n_exp - 1)
-            def _():
-                left = dot(pick_tail[...], gath[c].reshape(row_count, width)).astype(BF)
-                tail[c // 2, me, :, pl.ds(pl.multiple_of((c % 2) * width, width), width)] = left
+            @pl.when(jnp.logical_and(t >= units - 1 - pairs // 2, t < units - 1))
+            def _():
+                hoist(t - (units - 1 - pairs // 2) + pairs // 2)
 
         with scope("score"):
-            @pl.when(t >= 3 * parts)
+            @pl.when(jnp.logical_and(t >= 3 * parts - 1, t < units - 1))
             def _():
                 for v in range(2):
-                    u = 2 * (t - 3 * parts) + v
+                    u = 2 * (t - 3 * parts + 1) + v
                     x_take(u, n_stage)
                     scores(u)
+
+        with scope("xpass"):
+            for at, todo in FIRST_STEPS.items():
+                @pl.when(t == at)
+                def _(todo=todo):
+                    for u, stage in todo:
+                        x_pass(u, stage)
+
+            @pl.when(t > parts)
+            def _():
+                x_pass(t - LAG_FIRST, 1)
+
+            @pl.when(t >= parts + LAG_SECOND)
+            def _():
+                x_pass(t - LAG_SECOND, 2)
 
         return 0
 
@@ -668,7 +744,7 @@
         return pltpu.make_async_remote_copy(
             src_ref=agg.at[i],
             dst_ref=got.at[i],
-            send_sem=as_sem.at[i],
+            send_sem=as_sem,
             recv_sem=ar_sem.at[i],
             device_id={"seq": flip(me, order[i])},
         )
@@ -693,48 +769,32 @@
             agg[i + 1] = first + jnp.exp(first_t) * second
             a_copy(i + 1).start()
 
-    def mail_copy(other, source, slot):
-        return pltpu.make_async_remote_copy(
-            src_ref=mail.at[other // n_exp, turn_of(z, lax.rem(other, n_exp)) // 2],
-            dst_ref=inbox.at[source],
-            send_sem=ms_sem.at[slot],
-            recv_sem=mr_sem.at[source],
-            device_id={"seq": other // n_exp, "exp": lax.rem(other, n_exp)},
-        )
-
-    def post(i, _):
-        other = lax.rem(mine_id + i, n_dev)
-        mail_copy(other, mine_id, other).start()
-        return 0
-
-    def take(i, _):
-        other = lax.rem(mine_id + i, n_dev)
-        mail_copy(other, other, other).wait_recv()
-        return 0
-
-    def posted(i, _):
-        other = lax.rem(mine_id + i, n_dev)
-        mail_copy(other, mine_id, other).wait_send()
-        return 0
+    def post():
+        for i in reversed(range(n_exp)):
+            for apart in reversed(range(n_seq)):
+                if i == 0 and apart == 0:
+                    continue
+                target = me
+                for bit in order:
+                    if apart & bit:
+                        target = flip(target, bit)
+                pltpu.make_async_remote_copy(
+                    src_ref=mail.at[target, i // 2],
+                    dst_ref=inbox.at[mine_id],
+                    send_sem=ms_sem,
+                    recv_sem=mr_sem,
+                    device_id={"seq": target, "exp": nearest(z, i)},
+                ).start()
+
+    def finish(i):
+        def one(s, _):
+            both = jnp.transpose(acc[s, 2 * i : 2 * i + 2].reshape(2 * main, 128))
+            mail[s, i, 0:1, :] = jnp.sum(both, axis=0, keepdims=True)
+            return 0
+
+        lax.fori_loop(0, n_seq, one, 0, unroll=True)
 
     done = [2 * parts]
-
-    def pace(stage):
-        with scope("p%d" % stage):
-            if stage == 0:
-                x_start(None, 0)
-                x_pass(units - 2, 1)
-            if stage == 1:
-                x_pass(units - 4, 2)
-                x_pass(units - 1, 1)
-                x_pass(None, 1)
-            if stage == 2:
-                x_pass(units - 3, 2)
-            if stage == 3:
-                x_pass(units - 2, 2)
-            if stage == 4:
-                x_pass(units - 1, 2)
-                x_pass(None, 2)
 
     def count(upto):
         with scope("c%d" % upto):
@@ -743,82 +803,113 @@
                 scores(u)
             done[0] = max(done[0], upto)
 
-    pace(0)
+    def within(first, last):
+        with scope("within%d" % first):
+            lax.fori_loop(first * pairs // 8, last * pairs // 8, within_step, 0)
+
     with scope("state"):
         lax.fori_loop(0, pairs, state_step, 0)
         a_copy(0).start()
-    pace(1)
-    with scope("within1"):
-        lax.fori_loop(0, pairs // 4, within_step, 0)
-    pace(2)
+    with scope("pb"):
+        x_pass(units - 1, 1)
+        t_pass(1, 1)
+    within(0, 2)
+    with scope("pc"):
+        x_pass(units - 3, 2)
+        t_pass(0, 2)
     with scope("comb0"):
         combine(0)
-    count(units - 4)
-    pace(3)
-    with scope("within2"):
-        lax.fori_loop(pairs // 4, pairs // 2, within_step, 0)
-    pace(4)
-    with scope("comb1"):
-        combine(1)
+    count(units - 3)
+    with scope("pc2"):
+        x_pass(units - 2, 2)
+    within(2, 3)
+    with scope("finish0"):
+        for i in range(n_exp // 2 - 1):
+            finish(i)
+    with scope("pd"):
+        x_pass(units - 1, 2)
+        t_pass(1, 2)
+    count(units - 1)
     count(units)
     with scope("tailscore"):
-        x_take(None, n_stage)
+        for half in range(2):
+            t_take(half, n_stage)
         tail_scores()
-
-    with scope("finish"):
+    with scope("finish1"):
+        finish(n_exp // 2 - 1)
         wide = jnp.transpose(acc_tail[...].reshape(n_seq // 2 * extra * 2 * n_exp, 128))
         wide = jnp.sum(wide, axis=0, keepdims=True)
         wide = jnp.concatenate([wide, jnp.zeros((1, 128 - wide.shape[1]), F32)], axis=1)
-
-        def finish(s, _):
+        for s in range(n_seq):
             for i in range(n_exp // 2):
-                both = jnp.transpose(acc[s, 2 * i : 2 * i + 2].reshape(2 * main, 128))
-                mail[s, i, 0:1, :] = jnp.sum(both, axis=0, keepdims=True)
                 mail[s, i, 1:2, :] = wide
-            return 0
-
-        lax.fori_loop(0, n_seq, finish, 0)
     with scope("post"):
-        lax.fori_loop(1, n_dev, post, 0)
+        post()
         inbox[mine_id] = mail[me, 0]
 
-    with scope("within3"):
-        lax.fori_loop(pairs // 2, pairs, within_step, 0)
+    with scope("comb1"):
+        combine(1)
+    within(3, 8)
     with scope("comb2"):
         combine(2)
     with scope("out"):
         for i in range(blocks):
             lo, hi = i * block, (i + 1) * block
-            from_carry = dot(b_t[lo:hi, :], carry[...], precision=highest)
-            out_ref[lo:hi, :] = (inner[lo:hi, :] + fac[lo:hi, :] * from_carry).astype(BF)
+            from_carry = read_state(lo, hi, carry[...])
+            out_buf[lo:hi, :] = (inner[lo:hi, :] + fac[lo:hi, :] * from_carry).astype(BF)
+            pltpu.make_async_copy(
+                out_buf.at[pl.ds(lo, block)], out_hbm.at[pl.ds(lo, block)], out_sem
+            ).start()
 
     with scope("drain"):
-        def x_drain(u, _):
-            x_sent(u)
-            return 0
-
-        lax.fori_loop(0, units, x_drain, 0)
-        x_sent(None)
-        for k in range(parts):
-            for d in range(n_exp - 1):
-                z_sent(k, d)
-        for i in range(len(order)):
-            a_copy(i).wait_send()
-            d_copy(i).wait_send()
+        settled(rows.at[:, pl.ds(0, n_seq - 1)], xs_sem.at[0])
+        settled(tail.at[:, pl.ds(0, n_seq - 1)], xs_sem.at[1])
+        for d in range(n_exp - 1):
+            z_sent(d)
+        settled(agg, as_sem)
+        settled(span_sum, ds_sem)
     with scope("mail"):
-        lax.fori_loop(1, n_dev, take, 0)
+        settled(inbox.at[pl.ds(0, n_dev - 1)], mr_sem)
     with scope("gate"):
         for e in range(n_exp):
             total = inbox[e]
             for i in range(1, n_seq):
                 total = total + inbox[i * n_exp + e]
             vals[2 * e : 2 * e + 2, :] = total
+        first, rest = halves(vals[...])
+        second, third = halves(vals[...] - first.astype(F32))
+        split = jnp.concatenate([first, second, third, third], axis=0)
+        found = dot(split, where_at[...])
+        found = found[: 2 * n_exp] + found[2 * n_exp : 4 * n_exp] + found[4 * n_exp : 6 * n_exp]
         for k in range(ids_ref.shape[0]):
-            at = lax.broadcasted_iota(jnp.int32, (128, tok), 0) == spot[k : k + 1, :]
-            found = dot(vals[...], jnp.where(at, 1.0, 0.0), precision=highest)
-            pickd = lax.broadcasted_iota(jnp.int32, (2 * n_exp, tok), 0) == spot[2 + k : 3 + k, :]
-            gate_ref[k : k + 1, :] = jnp.sum(jnp.where(pickd, found, 0.0), axis=0, keepdims=True)
-        lax.fori_loop(1, n_dev, posted, 0)
+            named = lax.broadcasted_iota(jnp.int32, (2 * n_exp, tok), 0) == spot[k : k + 1, :]
+            value = jnp.where(named, found[:, k * tok : (k + 1) * tok], 0.0)
+            gate_ref[k : k + 1, :] = jnp.sum(value, axis=0, keepdims=True)
+        settled(inbox.at[pl.ds(0, n_dev - 1)], ms_sem)
+        pltpu.make_async_copy(out_buf, out_hbm, out_sem).wait()
+
+
+def pass_on(wide_in, gate_in, wide_out, gate_out, wide, gate, come, go):
+    strips = come.shape[0] - 1
+    size = wide.shape[0] // strips
+
+    def parts_of(i):
+        if i == strips:
+            return gate_in, gate, gate_out
+        span = pl.ds(i * size, size)
+        return wide_in.at[span], wide.at[span], wide_out.at[span]
+
+    def move(i, leg):
+        refs = parts_of(i)
+        return pltpu.make_async_copy(refs[leg], refs[leg + 1], (come, go)[leg].at[i])
+
+    for i in range(strips + 1):
+        move(i, 0).start()
+    for i in range(strips + 1):
+        move(i, 0).wait()
+        move(i, 1).start()
+    for i in range(strips + 1):
+        move(i, 1).wait()
 
 
 def plan(n_seq, n_exp, tok, depth, channels, cap, hidden, state, top):
@@ -840,11 +931,11 @@
         ((parts, channels, width), BF),
         ((cap, groups, hidden), BF),
         ((parts, hidden, width), BF),
-        ((512, hidden), BF),
+        ((512 + extra * groups, hidden), BF),
         ((parts, groups, main, width), F32),
         ((parts, extra, groups, width), F32),
         ((2 * units, n_seq, main, width // 2), BF),
-        ((2, n_seq, 16, depth // 2), BF),
+        ((2, n_seq, 2 * n_exp, depth // 2), BF),
         ((n_exp, main, tok), BF),
         ((16, row_count), BF),
         ((row_count, channels), F32),
@@ -869,6 +960,15 @@
         ((n_seq, n_exp // 2, 2, 128), F32),
         ((groups, 2, 128), F32),
         ((2 * n_exp, 128), F32),
+        ((row_count, channels), BF),
+        ((128, top * tok), BF),
+        ((heads, row_count), F32),
+        ((heads, row_count), F32),
+        ((state, row_count), F32),
+        ((state, row_count), F32),
+        ((1, channels), F32),
+        ((top, row_count), jnp.int32),
+        ((row_count, 3 * state), BF),
     ]
     total = 0
     for shape, kind in shapes:
@@ -877,7 +977,7 @@
             size *= extent
         total += size * (2 if kind is BF else 4)
     fits = (
-        total < VMEM_ROOM - (4 << 20)
+        total < VMEM_ROOM - (3 << 20)
         and n_seq & (n_seq - 1) == 0
         and stages == 3
         and n_exp == 4
@@ -887,16 +987,16 @@
         and top == 2
         and depth % (256 * parts) == 0
         and channels % (2 * HEAD) == 0
-        and pairs <= units // 2
+        and pairs == 8
         and row_count % block == 0
         and tok == 128
     )
     sems = [
-        (parts,), (), (parts,), (parts,),
-        (2, parts, steps), (2, parts, steps),
-        (2 * units + 2, n_seq - 1), (2 * units + 2, n_seq - 1),
-        (stages,), (stages,), (stages,), (stages,),
-        (groups,), (groups,),
+        (10,),
+        (2, steps), (2, parts, steps),
+        (2,), (units + 2, stages),
+        (), (stages,), (), (stages,),
+        (), (), (),
     ]
     return fits, (n_seq, n_exp, tok, cap, parts, width), shapes, sems
 
@@ -910,14 +1010,14 @@
     vmem = pl.BlockSpec(memory_space=pltpu.VMEM)
     hbm = pl.BlockSpec(memory_space=pl.ANY)
     row_count, channels = n_exp * tok, out_proj.shape[0]
-    return pl.pallas_call(
+    d_inner, d_gate = pl.pallas_call(
         functools.partial(fused, sizes),
         out_shape=(
             jax.ShapeDtypeStruct((row_count, channels), BF),
             jax.ShapeDtypeStruct((expert_ids.shape[1], tok), F32),
         ),
-        in_specs=[hbm] * 4 + [vmem] * 6,
-        out_specs=(vmem, vmem),
+        in_specs=[hbm] * 10,
+        out_specs=(hbm, vmem),
         scratch_shapes=[pltpu.VMEM(shape, kind) for shape, kind in shapes]
         + [pltpu.SemaphoreType.DMA(s) if s else pltpu.SemaphoreType.DMA for s in sems],
         compiler_params=pltpu.CompilerParams(
@@ -927,6 +1027,19 @@
         grad_out, out_proj, hidden_act.transpose(0, 2, 1, 3), w_down, step_size, log_decay, b_input, c_output,
         skip_gain.reshape(1, -1), expert_ids.T,
     )
+    return pl.pallas_call(
+        pass_on,
+        out_shape=(
+            jax.ShapeDtypeStruct(d_inner.shape, BF),
+            jax.ShapeDtypeStruct(d_gate.shape, F32),
+        ),
+        in_specs=[hbm] * 2,
+        out_specs=(hbm, hbm),
+        scratch_shapes=[
+            pltpu.VMEM(d_inner.shape, BF), pltpu.VMEM(d_gate.shape, F32),
+            pltpu.SemaphoreType.DMA((5,)), pltpu.SemaphoreType.DMA((5,)),
+        ],
+    )(d_inner, d_gate)
 
 
 def route(*args):

time: 72.1 us -> 59.1 us (0.82)
  Pallas kernels: 67.7 us -> 58.3 us
  local copies, waits for them, and re-layouts: 3.5 us -> 0 us
    pallas_call x1, Pallas kernels: 67.7 us -> 56.3 us  [quick(): pl.pallas_call(functools.partial(fused, sizes), out_shape=(jax.ShapeDtype...]
    unnamed x2 -> x0, local copies, waits for them, and re-layouts: 3.5 us -> none
    pallas_call x0 -> x1, Pallas kernels: none -> 2 us  [quick(): pl.pallas_call(pass_on, out_shape=(jax.ShapeDtypeStruct(d_inner.shape, BF...]
where the time goes in v2:
time: 59.1 us; the launch traced here: 58.9 us
  Pallas kernels  58.3 us (99%)
  between operations  0.64 us (1%)
    pallas_call x1, Pallas kernels, quick(): pl.pallas_call(functools.partial(fused, sizes), out_shape=(jax.ShapeDtype...  56.3 us
    pallas_call x1, Pallas kernels, quick(): pl.pallas_call(pass_on, out_shape=(jax.ShapeDtypeStruct(d_inner.shape, BF...  2 us

profile of v2, /device:TPU:0, one launch (start us, length us, event | category | flops | bytes accessed | tf_op | source)
XLA Modules:
  0.0 58.9 jit_solution(9369087898517089840)
XLA Ops:
  0.6 56.3 %shard_map.113 = (bf16[512,1024]{1,0:T(8,128)(2,1)}, f32[2,128]{1,0:T(2,128)}) custom-call(bf16[128,2048]{1,0:T(8,128)(2,1)} %grad_hbm.1, bf16[1024,2048]{1,0:T(8,128)(2,1)} %proj_hbm.1, bf16[1,66,32,1024]{3,2,1,0:T(8,128)(2,1)} %bitcast.3, bf16[1,1024,2048]{2,1,0:T(8,128)(2,1)} %down_hbm.1, f32[16,512]{1,0:T(8,128)} %step_hbm.1, f32[16,512]{1,0:T(8,128)} %decay_hbm.1, ...), custom_call_target="tpu_custom_call" | custom-call | tf_op jit(solution)/shard_map/pallas_call | solution.py:1013
  56.9 2.0 %shard_map.114 = (bf16[512,1024]{1,0:T(8,128)(2,1)}, f32[2,128]{1,0:T(2,128)}) custom-call(bf16[512,1024]{1,0:T(8,128)(2,1)} %get-tuple-element.4.wide_in, f32[2,128]{1,0:T(2,128)} %get-tuple-element.5.gate_in), custom_call_target="tpu_custom_call" | custom-call | tf_op jit(solution)/shard_map/pallas_call | solution.py:1030

commit v3 on v2

--- a/solution.py
+++ b/solution.py
@@ -166,14 +166,8 @@
 F32 = jnp.float32
 LAG_FIRST = 1
 LAG_SECOND = 3
-FIRST_STEPS = {
-    0: ((0, 1),),
-    1: ((1, 1), (2, 1)),
-    2: ((3, 1), (0, 2)),
-    3: ((1, 2),),
-    4: ((2, 2),),
-    5: ((3, 2),),
-}
+LAG_THIRD = 5
+RING = 8
 scope = jax.named_scope
 
 
@@ -371,12 +365,12 @@
                     src_ref=ref,
                     dst_ref=ref,
                     send_sem=xs_sem.at[0],
-                    recv_sem=xr_sem.at[u, stage],
+                    recv_sem=xr_sem.at[u % RING, stage],
                     device_id={"seq": flip(me, bit_of(half, stage))},
                 ).start()
 
     def x_take(u, stage):
-        settled(rows.at[pl.ds(2 * u, 2), pl.ds(0, 1 << stage)], xr_sem.at[u, stage])
+        settled(rows.at[pl.ds(2 * u, 2), pl.ds(0, 1 << stage)], xr_sem.at[u % RING, stage])
 
     def x_pass(u, stage):
         x_take(u, stage - 1)
@@ -389,12 +383,12 @@
                 src_ref=ref,
                 dst_ref=ref,
                 send_sem=xs_sem.at[1],
-                recv_sem=xr_sem.at[units + half, stage],
+                recv_sem=xr_sem.at[RING + half, stage],
                 device_id={"seq": flip(me, bit_of(half, stage))},
             ).start()
 
     def t_take(half, stage):
-        settled(tail.at[half, pl.ds(0, 1 << stage)], xr_sem.at[units + half, stage])
+        settled(tail.at[half, pl.ds(0, 1 << stage)], xr_sem.at[RING + half, stage])
 
     def t_pass(half, stage):
         t_take(half, stage - 1)
@@ -627,23 +621,35 @@
             down_load(k).start()
         for k in range(parts):
             proj_load(k).start()
+    with scope("prepare"):
+        prepare()
+        d_copy(0).start()
+    early = pairs // 2
+    hoisted = 0
+    for u in range(parts - 1):
+        with scope("hoist0"):
+            share = early - (parts - 2) if u == 0 else 1
+            for _ in range(share):
+                if hoisted < early:
+                    hoist(hoisted)
+                    hoisted += 1
+        with scope("early%d" % u):
+            x_pass(u, 1)
+    for j in range(hoisted, early):
+        hoist(j)
 
     def unit_step(t, _):
         i, c = t // parts, t % parts
 
         with scope("ztake"):
-            @pl.when(i >= 1)
-            def _():
-                z_take(c, i)
-
-            @pl.when(jnp.logical_and(i >= 1, i < n_exp - 1))
+            z_take(c, i)
+
+            @pl.when(i < n_exp - 1)
             def _():
                 z_send(c, i)
 
         with scope("pick"):
-            @pl.when(i >= 1)
-            def _():
-                choose(t, nearest(z, i), c)
+            choose(t, nearest(z, i), c)
 
         with scope("tailrows"):
             @pl.when(i == n_exp - 1)
@@ -661,38 +667,39 @@
             def _():
                 t_pass(0, 1)
 
-        with scope("hoist0"):
-            @pl.when(jnp.logical_and(t >= 1, t <= 2))
-            def _():
-                for v in range(pairs // 4):
-                    hoist((t - 1) * (pairs // 4) + v)
+        with scope("xsoon"):
+            @pl.when(jnp.logical_and(t > 3 * parts, t < units - 1))
+            def _():
+                x_pass(t - LAG_FIRST, 1)
 
         with scope("once"):
-            @pl.when(t == 0)
-            def _():
-                prepare()
-                d_copy(0).start()
-                settle()
-
-            @pl.when(t == parts - 1)
-            def _():
+            @pl.when(t == parts)
+            def _():
+                x_pass(parts - 1, 1)
                 hid_copy.wait()
                 settled(down, load_sem.at[1])
                 settled(proj, load_sem.at[2])
 
+            @pl.when(t == 2 * parts)
+            def _():
+                settle()
+
             for i_ in range(len(order)):
-                @pl.when(t == 2 * i_ + 3)
+                @pl.when(t == parts + 1 + 2 * i_)
                 def _(i_=i_):
                     d_copy(i_).wait_recv()
                     if i_ + 1 < len(order):
                         span_sum[i_ + 1] = span_sum[i_] + span_got[i_]
+                        if i_ == 1:
+                            span_sum[2, 1:2, :] = span_sum[1, 0:1, :]
+                            span_sum[2, 2:3, :] = span_got[1, 0:1, :]
                         d_copy(i_ + 1).start()
 
         with scope("project"):
-            @pl.when(jnp.logical_and(t >= parts - 1, t < 3 * parts - 1))
-            def _():
-                project(2 * (t - parts + 1))
-                project(2 * (t - parts + 1) + 1)
+            @pl.when(t < 3 * parts)
+            def _():
+                project(2 * (t - parts))
+                project(2 * (t - parts) + 1)
 
         with scope("inner"):
             @pl.when(i == n_exp - 1)
@@ -708,66 +715,89 @@
                     inner[...] += part
 
         with scope("hoist"):
-            @pl.when(jnp.logical_and(t >= units - 1 - pairs // 2, t < units - 1))
-            def _():
-                hoist(t - (units - 1 - pairs // 2) + pairs // 2)
+            @pl.when(jnp.logical_and(t < 3 * parts, t % 2 == 1))
+            def _():
+                hoist(early + (t - parts) // 2)
 
         with scope("score"):
-            @pl.when(jnp.logical_and(t >= 3 * parts - 1, t < units - 1))
+            @pl.when(jnp.logical_and(t >= 3 * parts, t < units - 1))
             def _():
                 for v in range(2):
-                    u = 2 * (t - 3 * parts + 1) + v
-                    x_take(u, n_stage)
-                    scores(u)
+                    scores(2 * (t - 3 * parts) + v)
 
         with scope("xpass"):
-            for at, todo in FIRST_STEPS.items():
-                @pl.when(t == at)
-                def _(todo=todo):
-                    for u, stage in todo:
-                        x_pass(u, stage)
-
-            @pl.when(t > parts)
+            @pl.when(jnp.logical_and(t > parts, t <= 3 * parts))
             def _():
                 x_pass(t - LAG_FIRST, 1)
 
+            @pl.when(t == units - 1)
+            def _():
+                x_pass(t - LAG_FIRST, 1)
+
+            @pl.when(t < 2 * parts)
+            def _():
+                x_pass(t - parts, 2)
+
             @pl.when(t >= parts + LAG_SECOND)
             def _():
                 x_pass(t - LAG_SECOND, 2)
 
+            @pl.when(t >= LAG_THIRD)
+            def _():
+                x_take(t - LAG_THIRD, n_stage)
+
         return 0
 
     with scope("unitloop"):
-        lax.fori_loop(0, units, unit_step, 0)
+        lax.fori_loop(parts, units, unit_step, 0)
+
+    reaches = [flip(me, bits[0]), flip(me, bits[1]), flip(flip(me, bits[0]), bits[1])]
 
     def a_copy(i):
         return pltpu.make_async_remote_copy(
-            src_ref=agg.at[i],
+            src_ref=agg.at[min(i, 1)],
             dst_ref=got.at[i],
-            send_sem=as_sem,
+            send_sem=as_sem.at[i],
             recv_sem=ar_sem.at[i],
-            device_id={"seq": flip(me, order[i])},
+            device_id={"seq": reaches[i - 1] if i else flip(me, 1)},
         )
 
-    reach = [jnp.zeros((1, channels), F32)]
-
-    def combine(i):
-        a_copy(i).wait_recv()
-        low = ((me // order[i]) % 2) == 0
-        other, other_t = got[i], span_got[i, 0:1, :]
-        own, own_t = agg[i], span_sum[i, 0:1, :]
-        added = jnp.where(low, jnp.exp(reach[0]) * other, 0.0)
-        if i == 0:
-            carry[...] = added
-        else:
-            carry[...] += added
-        reach[0] = reach[0] + jnp.where(low, other_t, 0.0)
-        if i + 1 < len(order):
-            first = jnp.where(low, own, other)
-            first_t = jnp.where(low, own_t, other_t)
-            second = jnp.where(low, other, own)
-            agg[i + 1] = first + jnp.exp(first_t) * second
-            a_copy(i + 1).start()
+    near_low = (me % 2) == 0
+    x_low = ((me // bits[0]) % 2) == 0
+    y_low = ((me // bits[1]) % 2) == 0
+
+    def combine():
+        a_copy(0).wait_recv()
+        other, other_t = got[0], span_got[0, 0:1, :]
+        own, own_t = agg[0], span_sum[0, 0:1, :]
+        carry[...] = jnp.where(near_low, other, 0.0)
+        first = jnp.where(near_low, own, other)
+        first_t = jnp.where(near_low, own_t, other_t)
+        second = jnp.where(near_low, other, own)
+        agg[1] = first + jnp.exp(first_t) * second
+        for i in (3, 2, 1):
+            @pl.when(reaches[i - 1] < me)
+            def _(i=i):
+                a_copy(i).start()
+
+    def combine_far():
+        reach = jnp.where(near_low, span_got[0, 0:1, :], 0.0)
+
+        @pl.when(x_low)
+        def _():
+            a_copy(1).wait_recv()
+            carry[...] += jnp.exp(reach) * got[1]
+
+        reach = reach + jnp.where(x_low, span_got[1, 0:1, :], 0.0)
+
+        @pl.when(y_low)
+        def _():
+            a_copy(2).wait_recv()
+            a_copy(3).wait_recv()
+            first = jnp.where(x_low, got[2], got[3])
+            first_t = jnp.where(x_low, span_got[2, 1:2, :], span_got[2, 2:3, :])
+            second = jnp.where(x_low, got[3], got[2])
+            carry[...] += jnp.exp(reach) * (first + jnp.exp(first_t) * second)
 
     def post():
         for i in reversed(range(n_exp)):
@@ -794,12 +824,13 @@
 
         lax.fori_loop(0, n_seq, one, 0, unroll=True)
 
-    done = [2 * parts]
+    done = [2 * (parts - 1)]
 
     def count(upto):
         with scope("c%d" % upto):
             for u in range(done[0], upto):
-                x_take(u, n_stage)
+                if u >= units - LAG_THIRD:
+                    x_take(u, n_stage)
                 scores(u)
             done[0] = max(done[0], upto)
 
@@ -813,12 +844,12 @@
     with scope("pb"):
         x_pass(units - 1, 1)
         t_pass(1, 1)
+    with scope("comb0"):
+        combine()
     within(0, 2)
     with scope("pc"):
         x_pass(units - 3, 2)
         t_pass(0, 2)
-    with scope("comb0"):
-        combine(0)
     count(units - 3)
     with scope("pc2"):
         x_pass(units - 2, 2)
@@ -847,11 +878,9 @@
         post()
         inbox[mine_id] = mail[me, 0]
 
-    with scope("comb1"):
-        combine(1)
     within(3, 8)
     with scope("comb2"):
-        combine(2)
+        combine_far()
     with scope("out"):
         for i in range(blocks):
             lo, hi = i * block, (i + 1) * block
@@ -866,7 +895,12 @@
         settled(tail.at[:, pl.ds(0, n_seq - 1)], xs_sem.at[1])
         for d in range(n_exp - 1):
             z_sent(d)
-        settled(agg, as_sem)
+        a_copy(0).wait_send()
+        for i in (3, 2, 1):
+            @pl.when(reaches[i - 1] < me)
+            def _(i=i):
+                a_copy(i).wait_send()
+
         settled(span_sum, ds_sem)
     with scope("mail"):
         settled(inbox.at[pl.ds(0, n_dev - 1)], mr_sem)
@@ -953,8 +987,8 @@
         ((max(blocks - 1, 1), state, channels), F32),
         ((stages, 8, channels), F32),
         ((stages, 8, channels), F32),
-        ((stages, state, channels), F32),
-        ((stages, state, channels), F32),
+        ((2, state, channels), F32),
+        ((stages + 1, state, channels), F32),
         ((state, channels), F32),
         ((8, tok), jnp.int32),
         ((n_seq, n_exp // 2, 2, 128), F32),
@@ -994,8 +1028,8 @@
     sems = [
         (10,),
         (2, steps), (2, parts, steps),
-        (2,), (units + 2, stages),
-        (), (stages,), (), (stages,),
+        (2,), (RING + 2, stages),
+        (), (stages,), (stages + 1,), (stages + 1,),
         (), (), (),
     ]
     return fits, (n_seq, n_exp, tok, cap, parts, width), shapes, sems

time: 59.1 us -> 58.2 us (0.985)
  Pallas kernels: 58.3 us -> 57.4 us
    pallas_call x1, Pallas kernels: 56.3 us -> 55.4 us  [quick(): pl.pallas_call(functools.partial(fused, sizes), out_shape=(jax.ShapeDtype...]
where the time goes in v3:
time: 58.2 us; the launch traced here: 58.1 us
  Pallas kernels  57.4 us (99%)
  between operations  0.64 us (1%)
    pallas_call x1, Pallas kernels, quick(): pl.pallas_call(functools.partial(fused, sizes), out_shape=(jax.ShapeDtype...  55.4 us
    pallas_call x1, Pallas kernels, quick(): pl.pallas_call(pass_on, out_shape=(jax.ShapeDtypeStruct(d_inner.shape, BF...  2 us

profile of v3, /device:TPU:0, one launch (start us, length us, event | category | flops | bytes accessed | tf_op | source)
XLA Modules:
  0.0 58.1 jit_solution(13568703695966204922)
XLA Ops:
  0.6 55.4 %shard_map.113 = (bf16[512,1024]{1,0:T(8,128)(2,1)}, f32[2,128]{1,0:T(2,128)}) custom-call(bf16[128,2048]{1,0:T(8,128)(2,1)} %grad_hbm.1, bf16[1024,2048]{1,0:T(8,128)(2,1)} %proj_hbm.1, bf16[1,66,32,1024]{3,2,1,0:T(8,128)(2,1)} %bitcast.3, bf16[1,1024,2048]{2,1,0:T(8,128)(2,1)} %down_hbm.1, f32[16,512]{1,0:T(8,128)} %step_hbm.1, f32[16,512]{1,0:T(8,128)} %decay_hbm.1, ...), custom_call_target="tpu_custom_call" | custom-call | tf_op jit(solution)/shard_map/pallas_call | solution.py:1047
  56.1 2.0 %shard_map.114 = (bf16[512,1024]{1,0:T(8,128)(2,1)}, f32[2,128]{1,0:T(2,128)}) custom-call(bf16[512,1024]{1,0:T(8,128)(2,1)} %get-tuple-element.4.wide_in, f32[2,128]{1,0:T(2,128)} %get-tuple-element.5.gate_in), custom_call_target="tpu_custom_call" | custom-call | tf_op jit(solution)/shard_map/pallas_call | solution.py:1064

commit v4 on v3

--- a/solution.py
+++ b/solution.py
@@ -857,9 +857,10 @@
     with scope("finish0"):
         for i in range(n_exp // 2 - 1):
             finish(i)
+    count(units - 2)
     with scope("pd"):
+        t_pass(1, 2)
         x_pass(units - 1, 2)
-        t_pass(1, 2)
     count(units - 1)
     count(units)
     with scope("tailscore"):

time: 58.2 us -> 58.2 us (level)
  no operation moved by 1% of the time
where the time goes in v4:
time: 58.2 us; the launch traced here: 58.1 us
  Pallas kernels  57.4 us (99%)
  between operations  0.64 us (1%)
    pallas_call x1, Pallas kernels, quick(): pl.pallas_call(functools.partial(fused, sizes), out_shape=(jax.ShapeDtype...  55.4 us
    pallas_call x1, Pallas kernels, quick(): pl.pallas_call(pass_on, out_shape=(jax.ShapeDtypeStruct(d_inner.shape, BF...  2 us

profile of v4, /device:TPU:0, one launch (start us, length us, event | category | flops | bytes accessed | tf_op | source)
XLA Modules:
  0.0 58.1 jit_solution(3068657180460964599)
XLA Ops:
  0.6 55.4 %shard_map.113 = (bf16[512,1024]{1,0:T(8,128)(2,1)}, f32[2,128]{1,0:T(2,128)}) custom-call(bf16[128,2048]{1,0:T(8,128)(2,1)} %grad_hbm.1, bf16[1024,2048]{1,0:T(8,128)(2,1)} %proj_hbm.1, bf16[1,66,32,1024]{3,2,1,0:T(8,128)(2,1)} %bitcast.3, bf16[1,1024,2048]{2,1,0:T(8,128)(2,1)} %down_hbm.1, f32[16,512]{1,0:T(8,128)} %step_hbm.1, f32[16,512]{1,0:T(8,128)} %decay_hbm.1, ...), custom_call_target="tpu_custom_call" | custom-call | tf_op jit(solution)/shard_map/pallas_call | solution.py:1048
  56.1 2.0 %shard_map.114 = (bf16[512,1024]{1,0:T(8,128)(2,1)}, f32[2,128]{1,0:T(2,128)}) custom-call(bf16[512,1024]{1,0:T(8,128)(2,1)} %get-tuple-element.4.wide_in, f32[2,128]{1,0:T(2,128)} %get-tuple-element.5.gate_in), custom_call_target="tpu_custom_call" | custom-call | tf_op jit(solution)/shard_map/pallas_call | solution.py:1065
